TPU v7x, 32 devices: a whole 2x2x4 slice. The times are simulated.
32 devices in a mesh: dp: 8 (over z, x), mp: 4 (over y, core).
Axes of the slice: x: 2, y: 2, z: 4, core: 2. Of those that a mesh axis runs over, the one named last changes fastest.
Arguments:
- latents: bfloat16 [16, 8, 32, 16], P('dp'), may hold values from -6 to 6
- gaussian_noise: float32 [16, 8, 32, 16], P('dp'), may hold values from -6 to 6
- timesteps: int32 [16], P('dp'), may hold values from 2 to 999, as said below
- counts: int32 [8], P('dp'), may hold values from 256 to 512, as said below
- captions: bfloat16 [16, 120, 4096], P('dp'), may hold values from -6 to 6
- w_in: float32 [20, 1152, 1152], P(None, 'dp'), may hold values from -0.1875 to 0.1875
- w_out: float32 [8, 1152, 1152], P(None, 'dp'), may hold values from -0.1875 to 0.1875
- w_cap: float32 [4096, 1152], P('dp'), may hold values from -0.09375 to 0.09375
- w_small: float32 [312, 1152], replicated, may hold values from -0.1875 to 0.1875
- rows_in: float32 [20, 1152], P(None, 'dp'), may hold values from 0 to 1
- cols_in: float32 [20, 1152], replicated, may hold values from 0 to 1
- rows_out: float32 [8, 1152], P(None, 'dp'), may hold values from 0 to 1
- cols_out: float32 [8, 1152], replicated, may hold values from 0 to 1
- rows_cap: float32 [4096], P('dp'), may hold values from 0 to 1
- cols_cap: float32 [1152], replicated, may hold values from 0 to 1
- rows_small: float32 [312], replicated, may hold values from 0 to 1
- cols_small: float32 [1152], replicated, may hold values from 0 to 1
Outputs:
- loss_mean: float32 [], replicated
- new_in: float32 [20, 1152, 1152], P(None, 'dp')
- copy_in: bfloat16 [20, 1152, 1152], P(None, 'dp')
- update_in: float32 [20, 1152, 1152], P(None, 'dp')
- new_rows_in: float32 [20, 1152], P(None, 'dp')
- new_cols_in: float32 [20, 1152], replicated
- new_out: float32 [8, 1152, 1152], P(None, 'dp')
- copy_out: bfloat16 [8, 1152, 1152], P(None, 'dp')
- update_out: float32 [8, 1152, 1152], P(None, 'dp')
- new_rows_out: float32 [8, 1152], P(None, 'dp')
- new_cols_out: float32 [8, 1152], replicated
- new_cap: float32 [4096, 1152], P('dp')
- copy_cap: bfloat16 [4096, 1152], P('dp')
- update_cap: float32 [4096, 1152], P('dp')
- new_rows_cap: float32 [4096], P('dp')
- new_cols_cap: float32 [1152], replicated
- new_small: float32 [312, 1152], replicated
- copy_small: bfloat16 [312, 1152], replicated
- update_small: float32 [312, 1152], replicated
- new_rows_small: float32 [312], replicated
- new_cols_small: float32 [1152], replicated
- spreads: float32 [30], replicated
Inputs may be any that keep to these rules, and one draw needn't show every extreme that they name: The samples of group g (rows g * 2 to g * 2 + 1) have timesteps from 2 + g * 124 to 1 + (g + 1) * 124. Each count is a multiple of 256; slots beyond counts are padding; some group is full and some holds one sample.
All inputs are finite; a program needn't handle non-finite values.
Results may differ from a plain program's by a relative error of at most 0.018.
The roundings to bfloat16 on the way count: a program that leaves them out, or rounds other values in their place, can miss the bound.
Values may be sent and summed in bfloat16 or wider, within the bound.
A program may use at most 320 MiB of HBM per device.

v0:
```python
import math

import jax
import jax.numpy as jnp
from jax import lax
from jax.sharding import PartitionSpec as P

HEAD_DIM = 72
D = 1152
FREQ = 256
CAP_DIM = 4096
CAP_LEN = 120
FRAMES = 8
GRID_H = 4
GRID_W = 8
PATCHES = 32
SLOTS = 2
STEP = 20
TOK_DEV = 512


norm_eps = 1e-06
relative_rate = 0.5
tanh_coeff = math.sqrt(2.0 / math.pi)
angle_unit = math.pi / 2.0 / 1.008 / 1000.0


def product(left, right):
    return jnp.dot(left, right, preferred_element_type=jnp.float32)


def contract(form, left, right):
    return jnp.einsum(form, left, right, preferred_element_type=jnp.float32)


def gelu_tanh(values):
    return (
        0.5 * values * (1.0 + jnp.tanh(tanh_coeff * (values + 0.044715 * values * values * values)))
    )


def layer_norm(values):
    center = values - jnp.mean(values, axis=-1, keepdims=True)
    return center * lax.rsqrt(jnp.mean(center * center, axis=-1, keepdims=True) + norm_eps)


def modulate(hidden, shift_rows, scale_rows):
    return layer_norm(hidden) * (1.0 + scale_rows) + shift_rows


def modulate_grad(hidden, shift_rows, scale_rows, grad_rows):
    pullback = jax.vjp(modulate, hidden, shift_rows, scale_rows)[1]
    return pullback(grad_rows)


def act_grad(function, values, grad_rows):
    return jax.vjp(function, values)[1](grad_rows)[0]


def sincos(positions, table_width):
    half_width = table_width // 2
    frequency = jnp.exp(
        -math.log(10000.0) * jnp.arange(half_width).astype(jnp.float32) / half_width
    )
    angles = positions[:, None] * frequency[None, :]
    return jnp.concatenate([jnp.sin(angles), jnp.cos(angles)], axis=1)


def position_tables():
    patch_index = jnp.arange(GRID_H * GRID_W)
    spatial = jnp.concatenate(
        [
            sincos((patch_index // GRID_W).astype(jnp.float32), D // 2),
            sincos((patch_index % GRID_W).astype(jnp.float32), D // 2),
        ],
        axis=1,
    )
    temporal = sincos(jnp.arange(FRAMES).astype(jnp.float32), D)
    return (spatial, temporal)


def time_features(timesteps):
    half_width = FREQ // 2
    frequency = jnp.exp(
        -math.log(10000.0) * jnp.arange(half_width).astype(jnp.float32) / half_width
    )
    angles = timesteps.astype(jnp.float32)[:, None] * frequency[None, :]
    return jnp.concatenate([jnp.cos(angles), jnp.sin(angles)], axis=1)


def plan(timesteps):
    moment = timesteps.astype(jnp.float32)
    start_angle = 8.0 * angle_unit
    cos_start = math.cos(start_angle) ** 2
    remain_now = jnp.sin((1000.0 - moment) * angle_unit)
    remain_before = jnp.sin((1001.0 - moment) * angle_unit)
    alpha_now = remain_now * remain_now / cos_start
    alpha_before = remain_before * remain_before / cos_start
    rest_now = (
        jnp.sin(2.0 * start_angle + moment * angle_unit) * jnp.sin(moment * angle_unit) / cos_start
    )
    rest_before = (
        jnp.sin(2.0 * start_angle + (moment - 1.0) * angle_unit)
        * jnp.sin((moment - 1.0) * angle_unit)
        / cos_start
    )
    beta_now = (
        jnp.sin(2.0 * start_angle + (2.0 * moment - 1.0) * angle_unit)
        * math.sin(angle_unit)
        / (remain_before * remain_before)
    )
    posterior = beta_now * rest_before / rest_now
    kappa = beta_now * beta_now * alpha_before / (rest_now * alpha_now)
    return (alpha_now, rest_now, beta_now, posterior, kappa)


def patch_terms(output, target, squared, beta_rows, posterior_rows, kappa_rows):
    error_rows = output[:, :, 0:4] - target
    log_beta = jnp.log(beta_rows)[:, None, None]
    log_post = jnp.log(posterior_rows)[:, None, None]
    fraction = (output[:, :, 4:8] + 1.0) * 0.5
    log_model = fraction * log_beta + (1.0 - fraction) * log_post
    diverge = 0.5 * (
        -1.0
        + log_model
        - log_post
        + jnp.exp(log_post - log_model)
        + kappa_rows[:, None, None] * squared * jnp.exp(-log_model)
    )
    return jnp.mean(error_rows * error_rows, axis=(1, 2)) + jnp.mean(
        diverge, axis=(1, 2)
    ) / math.log(2.0)


def to_frames(stacked, head_count):
    leading = stacked.shape[0]
    return (
        stacked.reshape(leading, SLOTS, FRAMES, PATCHES, head_count, HEAD_DIM)
        .transpose(0, 1, 3, 2, 4, 5)
        .reshape(leading, SLOTS * PATCHES, FRAMES, head_count, HEAD_DIM)
    )


def from_frames(stacked, head_count):
    leading = stacked.shape[0]
    return (
        stacked.reshape(leading, SLOTS, PATCHES, FRAMES, head_count, HEAD_DIM)
        .transpose(0, 1, 3, 2, 4, 5)
        .reshape(leading, SLOTS * FRAMES * PATCHES, head_count * HEAD_DIM)
    )


def attend_forward(queries, key_rows, value_rows):
    scores = contract("bqhc,bkhc->bhqk", queries, key_rows) * HEAD_DIM ** (-0.5)
    highest = jnp.max(scores, axis=-1, keepdims=True)
    shifted = jnp.exp(scores - highest)
    denominator = jnp.sum(shifted, axis=-1, keepdims=True)
    weights = (shifted / denominator).astype(jnp.bfloat16)
    return (contract("bhqk,bkhc->bqhc", weights, value_rows), highest + jnp.log(denominator))


def attend_backward(queries, key_rows, value_rows, logsum, grad_mixed):
    scores = contract("bqhc,bkhc->bhqk", queries, key_rows) * HEAD_DIM ** (-0.5)
    probability = jnp.exp(scores - logsum)
    grad_value = contract("bhqk,bqhc->bkhc", probability.astype(jnp.bfloat16), grad_mixed)
    grad_prob = contract("bqhc,bkhc->bhqk", grad_mixed, value_rows)
    grad_scores = (
        probability * (grad_prob - jnp.sum(probability * grad_prob, axis=-1, keepdims=True))
    ).astype(jnp.bfloat16)
    grad_query = contract("bhqk,bkhc->bqhc", grad_scores, key_rows) * HEAD_DIM ** (-0.5)
    grad_key = contract("bhqk,bqhc->bkhc", grad_scores, queries) * HEAD_DIM ** (-0.5)
    return (grad_query, grad_key, grad_value)


def branch_sum(pieces):
    return lax.psum(pieces, "mp")


def input_sum(pieces):
    return lax.psum(pieces, "mp")


def new_stat(old_stat, sums, length, inverse_sq):
    rho = 1.0 - STEP ** (-0.8)
    return rho * old_stat + (1.0 - rho) * (sums * inverse_sq / length + 1e-30)


def ratio_terms(weight, grad, rows_new, cols_new):
    ratio = jnp.sum(grad * grad / (rows_new[:, :, None] * cols_new[:, None, :]), axis=(1, 2))
    return jnp.stack([jnp.sum(rows_new, axis=1), ratio, jnp.sum(weight * weight, axis=(1, 2))])


def apply_update(weight, grad, rows_new, cols_new, mean_rows, spread, weight_scale):
    second = rows_new[:, :, None] * cols_new[:, None, :] / mean_rows[:, None, None]
    update = grad * lax.rsqrt(second)
    clipped = update / jnp.maximum(1.0, spread)[:, None, None]
    new_weight = weight - relative_rate * weight_scale[:, None, None] * clipped
    return (new_weight, new_weight.astype(jnp.bfloat16), clipped)


def shards(
    latents,
    gaussian_noise,
    timesteps,
    counts,
    captions,
    w_in,
    w_out,
    w_cap,
    w_small,
    rows_in,
    cols_in,
    rows_out,
    cols_out,
    rows_cap,
    cols_cap,
    rows_small,
    cols_small,
):
    bfloat = jnp.bfloat16
    mp_index = lax.axis_index("mp")
    local_width = w_in.shape[2] // lax.axis_size("mp")
    head_count = local_width // HEAD_DIM
    col_start = mp_index * local_width
    small_rows = 56 + FREQ
    in_cols = lax.dynamic_slice_in_dim(w_in[0:19], col_start, local_width, 2).astype(bfloat)
    out_cols = lax.dynamic_slice_in_dim(w_out, col_start, local_width, 2).astype(bfloat)
    cap_cols = lax.dynamic_slice_in_dim(w_cap, col_start, local_width, 1).astype(bfloat)
    full_in, temb_w, full_out, full_cap = (
        lax.all_gather(in_cols, "dp", axis=1, tiled=True),
        lax.all_gather(w_in[19].astype(bfloat), "dp", axis=0, tiled=True),
        lax.all_gather(out_cols, "dp", axis=1, tiled=True),
        lax.all_gather(cap_cols, "dp", axis=0, tiled=True),
    )
    full_small = w_small.astype(bfloat)
    per_sample = FRAMES * PATCHES
    patch_w = full_small[0:16]
    freq_w = full_small[16 : 16 + FREQ]
    tables = full_small[16 + FREQ : 24 + FREQ].astype(jnp.float32)
    final_w = full_small[24 + FREQ :]
    alpha_now, rest_now, beta_now, posterior, kappa = plan(timesteps)
    noisy_low = (
        jnp.sqrt(alpha_now)[:, None, None, None] * latents.astype(jnp.float32)
        + jnp.sqrt(rest_now)[:, None, None, None] * gaussian_noise
    ).astype(bfloat)
    patches = noisy_low.reshape(TOK_DEV, 16)
    spatial_pos, temporal_pos = position_tables()
    start_hidden = (
        product(patches, patch_w).reshape(SLOTS, FRAMES, PATCHES, D) + spatial_pos[None, None]
    ).reshape(SLOTS, per_sample, D)
    features = time_features(timesteps).astype(bfloat)
    first_pre = product(features, freq_w)
    first_act = jax.nn.silu(first_pre).astype(bfloat)
    time_emb = product(first_act, temb_w)
    temb_act = jax.nn.silu(time_emb).astype(bfloat)
    mod_local = contract("sd,kde->ske", temb_act, full_in[13:19])
    modulation = lax.all_gather(mod_local, "mp", axis=2, tiled=True) + tables[None, 0:6]
    shift_a, scale_a, gate_a, shift_b, scale_b, gate_b = [
        modulation[:, number][:, None, :] for number in range(6)
    ]
    cap_rows = captions.reshape(SLOTS * CAP_LEN, CAP_DIM)
    cap_mid = product(cap_rows, full_cap)
    cap_act = gelu_tanh(cap_mid).astype(bfloat)
    context_low = branch_sum(contract("re,de->rd", cap_act, full_out[7])).astype(bfloat)
    normed_a = modulate(start_hidden, shift_a, scale_a).astype(bfloat).reshape(TOK_DEV, D)
    qkv_s = (
        contract("td,kde->kte", normed_a, full_in[0:3])
        .astype(bfloat)
        .reshape(3, SLOTS * FRAMES, PATCHES, head_count, HEAD_DIM)
    )
    mixed_s, logsum_s = attend_forward(qkv_s[0], qkv_s[1], qkv_s[2])
    mixed_s_low = mixed_s.astype(bfloat).reshape(TOK_DEV, local_width)
    branch_s = branch_sum(contract("te,de->td", mixed_s_low, full_out[0])).reshape(
        SLOTS, per_sample, D
    )
    hidden_s = start_hidden + gate_a * branch_s
    timed_low = (
        (hidden_s.reshape(SLOTS, FRAMES, PATCHES, D) + temporal_pos[None, :, None, :])
        .astype(bfloat)
        .reshape(TOK_DEV, D)
    )
    qkv_t = to_frames(contract("td,kde->kte", timed_low, full_in[3:6]).astype(bfloat), head_count)
    mixed_t, logsum_t = attend_forward(qkv_t[0], qkv_t[1], qkv_t[2])
    mixed_t_low = from_frames(mixed_t.astype(bfloat)[None], head_count)[0]
    branch_t = branch_sum(contract("te,de->td", mixed_t_low, full_out[1])).reshape(
        SLOTS, per_sample, D
    )
    hidden_t = hidden_s + gate_a * branch_t
    hidden_low = hidden_t.astype(bfloat).reshape(TOK_DEV, D)
    query_c = (
        product(hidden_low, full_in[6])
        .astype(bfloat)
        .reshape(SLOTS, per_sample, head_count, HEAD_DIM)
    )
    key_value = (
        contract("rd,kde->kre", context_low, full_in[7:9])
        .astype(bfloat)
        .reshape(2, SLOTS, CAP_LEN, head_count, HEAD_DIM)
    )
    mixed_c, logsum_c = attend_forward(query_c, key_value[0], key_value[1])
    mixed_c_low = mixed_c.astype(bfloat).reshape(TOK_DEV, local_width)
    hidden_c = hidden_t + branch_sum(contract("te,de->td", mixed_c_low, full_out[2])).reshape(
        SLOTS, per_sample, D
    )
    normed_b = modulate(hidden_c, shift_b, scale_b).astype(bfloat).reshape(TOK_DEV, D)
    inner_pre = contract("td,kde->tke", normed_b, full_in[9:13])
    inner_act = gelu_tanh(inner_pre).astype(bfloat)
    branch_m = branch_sum(contract("tke,kde->td", inner_act, full_out[3:7])).reshape(
        SLOTS, per_sample, D
    )
    hidden_m = hidden_c + gate_b * branch_m
    shift_f = (tables[6] + time_emb)[:, None, :]
    scale_f = (tables[7] + time_emb)[:, None, :]
    normed_f = modulate(hidden_m, shift_f, scale_f).astype(bfloat).reshape(TOK_DEV, D)
    output = contract("td,od->to", normed_f, final_w).reshape(TOK_DEV, 4, 8)
    target = gaussian_noise.reshape(TOK_DEV, 4, 4)
    error_rows = output[:, :, 0:4] - target
    squared = error_rows * error_rows
    live_rows = jnp.repeat(
        (jnp.arange(SLOTS) * per_sample < counts[0]).astype(jnp.float32), per_sample
    )
    beta_rows = jnp.repeat(beta_now, per_sample)
    posterior_rows = jnp.repeat(posterior, per_sample)
    kappa_rows = jnp.repeat(kappa, per_sample)

    def patch_loss(values):
        return jnp.sum(
            patch_terms(values, target, squared, beta_rows, posterior_rows, kappa_rows) * live_rows
        )

    loss_local, loss_pull = jax.vjp(patch_loss, output)
    grad_output = loss_pull(jnp.ones_like(loss_local))[0].astype(bfloat).reshape(TOK_DEV, 32)
    grad_final = contract("to,td->od", grad_output, normed_f)
    grad_normed = contract("to,od->td", grad_output, final_w).reshape(SLOTS, per_sample, D)
    grad_hidden, grad_shift_f, grad_scale_f = modulate_grad(hidden_m, shift_f, scale_f, grad_normed)
    grad_gate_b = jnp.sum(grad_hidden * branch_m, axis=1)
    grad_branch = (gate_b * grad_hidden).astype(bfloat).reshape(TOK_DEV, D)
    grad_fc2 = contract("td,tke->kde", grad_branch, inner_act)
    grad_inner = act_grad(
        gelu_tanh, inner_pre, contract("td,kde->tke", grad_branch, full_out[3:7])
    ).astype(bfloat)
    grad_fc1 = contract("td,tke->kde", normed_b, grad_inner)
    grad_normed = input_sum(contract("tke,kde->td", grad_inner, full_in[9:13])).reshape(
        SLOTS, per_sample, D
    )
    grad_more, grad_shift_b, grad_scale_b = modulate_grad(hidden_c, shift_b, scale_b, grad_normed)
    grad_hidden = grad_hidden + grad_more
    grad_branch = grad_hidden.astype(bfloat).reshape(TOK_DEV, D)
    grad_cproj = contract("td,te->de", grad_branch, mixed_c_low)
    grad_mixed = (
        contract("td,de->te", grad_branch, full_out[2])
        .astype(bfloat)
        .reshape(SLOTS, per_sample, head_count, HEAD_DIM)
    )
    grad_query, grad_key, grad_value = attend_backward(
        query_c, key_value[0], key_value[1], logsum_c, grad_mixed
    )
    grad_query = grad_query.astype(bfloat).reshape(TOK_DEV, local_width)
    grad_kv = (
        jnp.stack([grad_key, grad_value]).astype(bfloat).reshape(2, SLOTS * CAP_LEN, local_width)
    )
    grad_cq = contract("td,te->de", hidden_low, grad_query)
    grad_ckv = contract("rd,kre->kde", context_low, grad_kv)
    grad_hidden = grad_hidden + input_sum(contract("te,de->td", grad_query, full_in[6])).reshape(
        SLOTS, per_sample, D
    )
    grad_context = input_sum(contract("kre,kde->rd", grad_kv, full_in[7:9])).astype(bfloat)
    grad_gate_a = jnp.sum(grad_hidden * branch_t, axis=1)
    grad_branch = (gate_a * grad_hidden).astype(bfloat).reshape(TOK_DEV, D)
    grad_tproj = contract("td,te->de", grad_branch, mixed_t_low)
    grad_mixed = to_frames(
        contract("td,de->te", grad_branch, full_out[1]).astype(bfloat)[None], head_count
    )[0]
    grads_t = attend_backward(qkv_t[0], qkv_t[1], qkv_t[2], logsum_t, grad_mixed)
    grad_qkv = from_frames(jnp.stack(grads_t).astype(bfloat), head_count)
    grad_tqkv = contract("td,kte->kde", timed_low, grad_qkv)
    grad_hidden = grad_hidden + input_sum(contract("kte,kde->td", grad_qkv, full_in[3:6])).reshape(
        SLOTS, per_sample, D
    )
    grad_gate_a = grad_gate_a + jnp.sum(grad_hidden * branch_s, axis=1)
    grad_branch = (gate_a * grad_hidden).astype(bfloat).reshape(TOK_DEV, D)
    grad_sproj = contract("td,te->de", grad_branch, mixed_s_low)
    grad_mixed = (
        contract("td,de->te", grad_branch, full_out[0])
        .astype(bfloat)
        .reshape(SLOTS * FRAMES, PATCHES, head_count, HEAD_DIM)
    )
    grads_s = attend_backward(qkv_s[0], qkv_s[1], qkv_s[2], logsum_s, grad_mixed)
    grad_qkv = jnp.stack(grads_s).astype(bfloat).reshape(3, TOK_DEV, local_width)
    grad_sqkv = contract("td,kte->kde", normed_a, grad_qkv)
    grad_normed = input_sum(contract("kte,kde->td", grad_qkv, full_in[0:3])).reshape(
        SLOTS, per_sample, D
    )
    grad_more, grad_shift_a, grad_scale_a = modulate_grad(
        start_hidden, shift_a, scale_a, grad_normed
    )
    grad_hidden = grad_hidden + grad_more
    grad_patch = contract("ti,td->id", patches, grad_hidden.astype(bfloat).reshape(TOK_DEV, D))
    grad_mods = jnp.stack(
        [
            grad_shift_a[:, 0],
            grad_scale_a[:, 0],
            grad_gate_a,
            grad_shift_b[:, 0],
            grad_scale_b[:, 0],
            grad_gate_b,
        ],
        axis=1,
    )
    grad_mods_low = lax.dynamic_slice_in_dim(grad_mods.astype(bfloat), col_start, local_width, 2)
    grad_temb_act = input_sum(contract("ske,kde->sd", grad_mods_low, full_in[13:19]))
    grad_temb = (
        act_grad(jax.nn.silu, time_emb, grad_temb_act) + grad_shift_f[:, 0] + grad_scale_f[:, 0]
    )
    grad_temb_low = grad_temb.astype(bfloat)
    grad_first = act_grad(
        jax.nn.silu, first_pre, contract("sd,id->si", grad_temb_low, temb_w)
    ).astype(bfloat)
    grad_tables = jnp.concatenate(
        [
            jnp.sum(grad_mods, axis=0),
            jnp.stack([jnp.sum(grad_shift_f[:, 0], axis=0), jnp.sum(grad_scale_f[:, 0], axis=0)]),
        ],
        axis=0,
    )
    grad_cap2 = contract("rd,re->de", grad_context, cap_act)
    grad_cap_mid = act_grad(
        gelu_tanh, cap_mid, contract("rd,de->re", grad_context, full_out[7])
    ).astype(bfloat)
    grad_cap = contract("rc,re->ce", cap_rows, grad_cap_mid)
    grad_in_head = jnp.concatenate(
        [grad_sqkv, grad_tqkv, grad_cq[None], grad_ckv, grad_fc1], axis=0
    )
    grad_out_all = jnp.concatenate(
        [grad_sproj[None], grad_tproj[None], grad_cproj[None], grad_fc2, grad_cap2[None]], axis=0
    )
    small_tail = jnp.concatenate([grad_tables, grad_final], axis=0)
    grad_time = contract("sd,ske->kde", temb_act, grad_mods_low)
    grad_temb_part = contract(
        "si,sd->id", first_act, lax.dynamic_slice_in_dim(grad_temb_low, col_start, local_width, 1)
    )
    grad_freq = contract("sf,sd->fd", features, grad_first)
    sum_in, sum_out, sum_cap = (
        lax.psum_scatter(
            jnp.concatenate([grad_in_head, grad_time, grad_temb_part[None]], axis=0).astype(
                jnp.bfloat16
            ),
            "dp",
            scatter_dimension=1,
            tiled=True,
        ).astype(jnp.float32),
        lax.psum_scatter(
            grad_out_all.astype(jnp.bfloat16), "dp", scatter_dimension=1, tiled=True
        ).astype(jnp.float32),
        lax.psum_scatter(
            grad_cap.astype(jnp.bfloat16), "dp", scatter_dimension=0, tiled=True
        ).astype(jnp.float32),
    )
    sum_small = lax.psum(
        jnp.concatenate([grad_patch, grad_freq, small_tail], axis=0).astype(jnp.bfloat16), "dp"
    ).astype(jnp.float32)
    sum_in, sum_out, sum_cap = (
        lax.all_gather(sum_in.astype(jnp.bfloat16), "mp", axis=2, tiled=True).astype(sum_in.dtype),
        lax.all_gather(sum_out.astype(jnp.bfloat16), "mp", axis=2, tiled=True).astype(
            sum_out.dtype
        ),
        lax.all_gather(sum_cap.astype(jnp.bfloat16), "mp", axis=1, tiled=True).astype(
            sum_cap.dtype
        ),
    )
    count_local = counts[0].astype(jnp.float32)
    square_in = sum_in * sum_in
    square_out = sum_out * sum_out
    square_cap = sum_cap * sum_cap
    square_small = sum_small * sum_small
    row_in_total = jnp.sum(square_in, axis=2)
    row_out_total = jnp.sum(square_out, axis=2)
    row_cap_total = jnp.sum(square_cap, axis=1)
    row_small_total = jnp.sum(square_small, axis=1)
    col_small_total = jnp.sum(square_small, axis=0)
    col_in_total, col_out_total, col_cap_total, loss_total, count_total = (
        lax.psum(jnp.sum(square_in, axis=1).astype(jnp.bfloat16), "dp").astype(jnp.float32),
        lax.psum(jnp.sum(square_out, axis=1).astype(jnp.bfloat16), "dp").astype(jnp.float32),
        lax.psum(jnp.sum(square_cap, axis=0).astype(jnp.bfloat16), "dp").astype(jnp.float32),
        lax.psum(loss_local.astype(jnp.bfloat16), "dp").astype(jnp.float32),
        lax.psum(count_local.astype(jnp.bfloat16), "dp").astype(jnp.float32),
    )
    inverse = 1.0 / count_total
    inverse_sq = inverse * inverse
    rows_in_new = new_stat(rows_in, row_in_total, D, inverse_sq)
    cols_in_new = new_stat(cols_in, col_in_total, D, inverse_sq)
    rows_out_new = new_stat(rows_out, row_out_total, D, inverse_sq)
    cols_out_new = new_stat(cols_out, col_out_total, D, inverse_sq)
    rows_cap_new = new_stat(rows_cap, row_cap_total, D, inverse_sq)
    cols_cap_new = new_stat(cols_cap, col_cap_total, CAP_DIM, inverse_sq)
    rows_small_new = new_stat(rows_small, row_small_total, D, inverse_sq)
    cols_small_new = new_stat(cols_small, col_small_total, small_rows, inverse_sq)
    grad_in = sum_in * inverse
    grad_out = sum_out * inverse
    grad_cap_all = (sum_cap * inverse)[None]
    grad_small_all = (sum_small * inverse)[None]
    ratios = lax.psum(
        jnp.concatenate(
            [
                ratio_terms(w_in, grad_in, rows_in_new, cols_in_new),
                ratio_terms(w_out, grad_out, rows_out_new, cols_out_new),
                ratio_terms(w_cap[None], grad_cap_all, rows_cap_new[None], cols_cap_new[None]),
            ],
            axis=1,
        ),
        "dp",
    )
    totals = jnp.concatenate(
        [
            ratios,
            ratio_terms(w_small[None], grad_small_all, rows_small_new[None], cols_small_new[None]),
        ],
        axis=1,
    )
    row_count = jnp.array([float(D)] * 28 + [float(CAP_DIM), float(small_rows)], jnp.float32)
    mean_rows = totals[0] / row_count
    spreads = jnp.sqrt(mean_rows * totals[1] / (row_count * D))
    weight_scale = jnp.sqrt(totals[2] / (row_count * D))
    in_new, in_copy, in_update = apply_update(
        w_in, grad_in, rows_in_new, cols_in_new, mean_rows[0:20], spreads[0:20], weight_scale[0:20]
    )
    out_new, out_copy, out_update = apply_update(
        w_out,
        grad_out,
        rows_out_new,
        cols_out_new,
        mean_rows[20:28],
        spreads[20:28],
        weight_scale[20:28],
    )
    cap_new, cap_copy, cap_update = apply_update(
        w_cap[None],
        grad_cap_all,
        rows_cap_new[None],
        cols_cap_new[None],
        mean_rows[28:29],
        spreads[28:29],
        weight_scale[28:29],
    )
    small_new, small_copy, small_update = apply_update(
        w_small[None],
        grad_small_all,
        rows_small_new[None],
        cols_small_new[None],
        mean_rows[29:30],
        spreads[29:30],
        weight_scale[29:30],
    )
    return (
        loss_total * inverse,
        in_new,
        in_copy,
        in_update,
        rows_in_new,
        cols_in_new,
        out_new,
        out_copy,
        out_update,
        rows_out_new,
        cols_out_new,
        cap_new[0],
        cap_copy[0],
        cap_update[0],
        rows_cap_new,
        cols_cap_new,
        small_new[0],
        small_copy[0],
        small_update[0],
        rows_small_new,
        cols_small_new,
        spreads,
    )


def solution(mesh):
    in_specs = (
        P("dp", None, None, None),
        P("dp", None, None, None),
        P("dp"),
        P("dp"),
        P("dp", None, None),
        P(None, "dp", None),
        P(None, "dp", None),
        P("dp", None),
        P(),
        P(None, "dp"),
        P(),
        P(None, "dp"),
        P(),
        P("dp"),
        P(),
        P(),
        P(),
    )
    out_specs = (
        P(),
        P(None, "dp", None),
        P(None, "dp", None),
        P(None, "dp", None),
        P(None, "dp"),
        P(),
        P(None, "dp", None),
        P(None, "dp", None),
        P(None, "dp", None),
        P(None, "dp"),
        P(),
        P("dp", None),
        P("dp", None),
        P("dp", None),
        P("dp"),
        P(),
        P(),
        P(),
        P(),
        P(),
        P(),
        P(),
    )
    return jax.shard_map(shards, mesh=mesh, in_specs=in_specs, out_specs=out_specs, check_vma=False)
```

profile of v0, /device:TPU:0, one launch (start us, length us, event | category | flops | bytes accessed | tf_op | source)
XLA Modules:
  0.0 2306.1 jit_solution(363245606751137548)
XLA Ops:
  38.2 30.3 %all-gather.21.cloned.1.call-done = bf16[1,1152,1152]{2,1,0:T(8,128)(2,1)} async-done(((bf16[1,144,1152]{2,1,0:T(8,128)(2,1)}), bf16[1,1152,1152]{2,1,0:T(8,128)(2,1)}) %all-gather.21.cloned.1.call-update) | async-done | bytes 2654224 | tf_op jit(solution)/shard_map/all_gather | solution.py:231
  71.4 106.8 %all-gather.11.cloned.1.call-done = bf16[8,1152,288]{2,0,1:T(8,128)(2,1)} async-done(((bf16[8,144,288]{2,0,1:T(8,128)(2,1)}), bf16[8,1152,288]{2,0,1:T(8,128)(2,1)}) %all-gather.11.cloned.1.call-update) | async-done | bytes 5308432 | tf_op jit(solution)/shard_map/all_gather | solution.py:232
  200.4 301.8 %all-gather.9.cloned.1.call-done = bf16[19,1152,288]{2,1,0:T(8,128)(2,1)} async-done(((bf16[19,144,288]{2,1,0:T(8,128)(2,1)}), bf16[19,1152,288]{2,1,0:T(8,128)(2,1)}) %all-gather.9.cloned.1.call-update) | async-done | bytes 12607504 | tf_op jit(solution)/shard_map/all_gather | solution.py:230
  536.3 28.6 %all-gather.13.cloned.1.call-done = bf16[4096,288]{1,0:T(8,128)(2,1)} async-done(((bf16[512,288]{1,0:T(8,128)(2,1)}), bf16[4096,288]{1,0:T(8,128)(2,1)}) %all-gather.13.cloned.1.call-update) | async-done | bytes 2359312 | tf_op jit(solution)/shard_map/all_gather | solution.py:233
  585.0 37.0 %all-reduce.17.cloned.1.call-done = f32[512,1152]{1,0:T(8,128)} async-done(((f32[512,1152]{1,0:T(8,128)}), f32[512,1152]{1,0:T(8,128)}) %all-reduce.17.cloned.1.call-update) | async-done | bytes 2359312 | tf_op jit(solution)/shard_map/psum | solution.py:176
  649.9 42.9 %all-reduce.34 = bf16[240,1152]{1,0:T(8,128)(2,1)} all-reduce(f32[240,1152]{1,0:T(8,128)} %fusion.133), channel_id=1, replica_groups=mesh['dp'=8,'mp'=4] {'mp'}, use_global_device_ids=true, to_apply=%region_8.9 | all-reduce | flops 276480 | bytes 1658880 | tf_op jit(solution)/shard_map/psum | solution.py:176
  699.4 22.7 all-reduce.19.cloned.1.call-done
  754.0 39.7 %all-reduce.21.cloned.1.call-done = f32[512,1152]{1,0:T(8,128)} async-done(((f32[512,1152]{1,0:T(8,128)}), f32[512,1152]{1,0:T(8,128)}) %all-reduce.21.cloned.1.call-update) | async-done | bytes 2359312 | tf_op jit(solution)/shard_map/psum | solution.py:176
  815.2 48.8 %all-reduce.23.cloned.1.call-done = f32[512,1152]{1,0:T(8,128)} async-done(((f32[512,1152]{1,0:T(8,128)}), f32[512,1152]{1,0:T(8,128)}) %all-reduce.23.cloned.1.call-update) | async-done | bytes 2359312 | tf_op jit(solution)/shard_map/psum | solution.py:176
  909.7 52.7 %all-reduce.25.cloned.1.call-done = f32[512,1152]{1,0:T(8,128)} async-done(((f32[512,1152]{1,0:T(8,128)}), f32[512,1152]{1,0:T(8,128)}) %all-reduce.25.cloned.1.call-update) | async-done | bytes 2359312 | tf_op jit(solution)/shard_map/psum | solution.py:180
  991.8 54.0 %all-reduce.27.cloned.1.call-done = f32[2,256,1152]{2,1,0:T(8,128)} async-done(((f32[2,256,1152]{2,1,0:T(8,128)}), f32[2,256,1152]{2,1,0:T(8,128)}) %all-reduce.27.cloned.1.call-update) | async-done | bytes 2359312 | tf_op jit(solution)/shard_map/psum | solution.py:180
  1077.4 54.5 %all-reduce.29.cloned.1.call-done = f32[2,256,1152]{2,1,0:T(8,128)} async-done(((f32[2,256,1152]{2,1,0:T(8,128)}), f32[2,256,1152]{2,1,0:T(8,128)}) %all-reduce.29.cloned.1.call-update) | async-done | bytes 2359312 | tf_op jit(solution)/shard_map/psum | solution.py:180
  1164.1 48.5 %all-reduce.31.cloned.1.call-done = f32[512,1152]{1,0:T(8,128)} async-done(((f32[512,1152]{1,0:T(8,128)}), f32[512,1152]{1,0:T(8,128)}) %all-reduce.31.cloned.1.call-update) | async-done | bytes 2359312 | tf_op jit(solution)/shard_map/psum | solution.py:180
  1227.5 27.2 %all-reduce.35 = (f32[2,1152]{1,0:T(2,128)S(1)}, bf16[240,1152]{1,0:T(8,128)(2,1)}) all-reduce(f32[2,1152]{1,0:T(2,128)S(1)} %fusion.85, f32[240,1152]{1,0:T(8,128)} %convolution_bitcast_fusion.3), channel_id=1, replica_groups=mesh['dp'=8,'mp'=4] {'mp'}, use_global_device_ids=true, to_apply=%region_40.41 | all-reduce | flops 278784 | bytes 1677312 | tf_op jit(solution)/shard_map/psum | solution.py:180
  1298.8 25.6 %copy.642 = bf16[20,1152,288]{2,0,1:T(8,128)(2,1)} copy(bf16[20,1152,288]{1,2,0:T(8,128)(2,1)} %fusion.44) | data formatting | bytes 26542080 | tf_op jit(solution)/shard_map/concatenate | solution.py:445
  1333.9 128.7 %reduce-scatter.6.cloned.1.call-done = bf16[8,144,288]{2,0,1:T(8,128)(2,1)} async-done(((bf16[8,1152,288]{2,0,1:T(8,128)(2,1)}), bf16[8,144,288]{2,0,1:T(8,128)(2,1)}) %reduce-scatter.6.cloned.1.call-update) | async-done | bytes 663568 | tf_op jit(solution)/shard_map/reduce_scatter | solution.py:452
  1466.1 346.1 %reduce-scatter.4.cloned.1.call-done = bf16[20,144,288]{2,0,1:T(8,128)(2,1)} async-done(((bf16[20,1152,288]{2,0,1:T(8,128)(2,1)}), bf16[20,144,288]{2,0,1:T(8,128)(2,1)}) %reduce-scatter.4.cloned.1.call-update) | async-done | bytes 1658896 | tf_op jit(solution)/shard_map/reduce_scatter | solution.py:444
  1819.3 26.5 %copy.656 = f32[20,144,1152]{1,0,2:T(8,128)} copy(f32[20,144,1152]{2,1,0:T(8,128)} %param.23) | data formatting | bytes 26542080 | tf_op args[5]
  1909.4 37.8 %all-gather.17.cloned.1.call-done = bf16[8,144,1152]{1,0,2:T(8,128)(2,1)} async-done(((bf16[8,144,288]{1,0,2:T(8,128)(2,1)}), bf16[8,144,1152]{1,0,2:T(8,128)(2,1)}) %all-gather.17.cloned.1.call-update) | async-done | bytes 2654224 | tf_op jit(solution)/shard_map/all_gather | solution.py:464
  1951.1 89.3 %all-gather.15.cloned.1.call-done = bf16[20,144,1152]{1,0,2:T(8,128)(2,1)} async-done(((bf16[20,144,288]{1,0,2:T(8,128)(2,1)}), bf16[20,144,1152]{1,0,2:T(8,128)(2,1)}) %all-gather.15.cloned.1.call-update) | async-done | bytes 6635536 | tf_op jit(solution)/shard_map/all_gather | solution.py:463
  2048.6 41.1 %all-reduce.36 = (bf16[]{:T(256)}, bf16[]{:T(256)}, bf16[1152]{0:T(1024)(128)(2,1)S(1)}, bf16[8,1152]{1,0:T(8,128)(2,1)S(1)}, bf16[20,1152]{0,1:T(8,128)(2,1)S(1)}) all-reduce(bf16[]{:T(256)} %multiply_reduce_fusion.18, bf16[]{:T(256)S(6)} %convert_element_type.365, ...), channel_id=1, replica_groups=mesh['dp'=8,'mp'=4] {'dp'}, use_global_device_ids=true, to_apply=%region_20.21 | all-reduce | flops 33410 | bytes 133640 | tf_op jit(solution)/shard_map/psum | solution.py:485
  2139.0 39.1 %fusion.247 = (bf16[20,144,1152]{1,0,2:T(8,128)(2,1)}, f32[20,144,1152]{1,0,2:T(8,128)}, f32[20,144,1152]{1,0,2:T(8,128)}) fusion(f32[20,144,1152]{1,0,2:T(8,128)} %copy.656, f32[20]{0:T(128)S(1)} %multiply_bitcast_fusion.1, f32[20]{0:T(128)S(1)} %maximum_bitcast_fusion.2, f32[20]{0:T(128)S(1)} %slice_bitcast_fusion.10, ...), kind=kLoop, calls=%fused_computation.477 | loop fusion | flops 29859840 | bytes 53188084 | tf_op jit(solution)/shard_map/convert_element_type | solution.py:198
  2178.1 22.6 copy.659
  2217.4 22.7 copy.661
  (660 shorter events, 609.1 us)
Async XLA Ops:
  7.2 557.7 %copy-start = (bf16[2,120,4096]{2,1,0:T(8,128)(2,1)S(1)}, bf16[2,120,4096]{2,1,0:T(8,128)(2,1)}, u32[]{:S(2)}) copy-start(bf16[2,120,4096]{2,1,0:T(8,128)(2,1)} %param.22) | copy-start | bytes 5898244
  7.2 61.3 %all-gather.21.cloned.1.call-start = ((), (), s32[]{:S(2)}) async-start(), calls=%async_computation.21 | async-start | bytes 2985984 | tf_op jit(solution)/shard_map/all_gather | solution.py:231
  9.3 168.9 %all-gather.11.cloned.1.call-start = ((), (), s32[]{:S(2)}) async-start(), calls=%async_computation.4 | async-start | bytes 7962624 | tf_op jit(solution)/shard_map/all_gather | solution.py:232
  12.4 489.8 %all-gather.9.cloned.1.call-start = ((), (), s32[]{:S(2)}) async-start(), calls=%async_computation.3 | async-start | bytes 18911232 | tf_op jit(solution)/shard_map/all_gather | solution.py:230
  24.8 540.1 %all-gather.13.cloned.1.call-start = ((), (), s32[]{:S(2)}) async-start(), calls=%async_computation.7 | async-start | bytes 3538944 | tf_op jit(solution)/shard_map/all_gather | solution.py:233
  27.2 594.8 %all-reduce.17.cloned.1.call-start = ((), (), s32[]{:S(2)}) async-start(), calls=%async_computation.5 | async-start | bytes 4718592 | tf_op jit(solution)/shard_map/psum | solution.py:176
  35.3 483.0 %copy-start.124 = (f32[512]{0:T(512)}, f32[512]{0:T(512)S(1)}, u32[]{:S(2)}) copy-start(f32[512]{0:T(512)S(1)} %div.346) | copy-start | bytes 6148
  37.4 480.9 %copy-start.128 = (f32[512]{0:T(512)}, f32[512]{0:T(512)S(1)}, u32[]{:S(2)}) copy-start(f32[512]{0:T(512)S(1)} %rsqrt.58) | copy-start | bytes 6148
  71.4 430.9 %copy-start.97 = (f32[2,1152]{1,0:T(2,128)}, f32[2,1152]{1,0:T(2,128)S(1)}, u32[]{:S(2)}) copy-start(f32[2,1152]{1,0:T(2,128)S(1)} %get-tuple-element.334) | copy-start | bytes 27652
  535.7 186.4 %all-reduce.19.cloned.1.call-start = ((), (), s32[]{:S(2)}) async-start(), calls=%async_computation.6 | async-start | bytes 4718592 | tf_op jit(solution)/shard_map/psum | solution.py:176
  649.9 143.8 %all-reduce.21.cloned.1.call-start = ((), (), s32[]{:S(2)}) async-start(), calls=%async_computation.8 | async-start | bytes 4718592 | tf_op jit(solution)/shard_map/psum | solution.py:176
  737.8 126.2 %all-reduce.23.cloned.1.call-start = ((), (), s32[]{:S(2)}) async-start(), calls=%async_computation.9 | async-start | bytes 4718592 | tf_op jit(solution)/shard_map/psum | solution.py:176
  808.1 154.3 %all-reduce.25.cloned.1.call-start = ((), (), s32[]{:S(2)}) async-start(), calls=%async_computation.10 | async-start | bytes 4718592 | tf_op jit(solution)/shard_map/psum | solution.py:180
  906.5 139.3 %all-reduce.27.cloned.1.call-start = ((), (), s32[]{:S(2)}) async-start(), calls=%async_computation.11 | async-start | bytes 4718592 | tf_op jit(solution)/shard_map/psum | solution.py:180
  989.9 142.0 %all-reduce.29.cloned.1.call-start = ((), (), s32[]{:S(2)}) async-start(), calls=%async_computation.12 | async-start | bytes 4718592 | tf_op jit(solution)/shard_map/psum | solution.py:180
  1076.0 136.6 %all-reduce.31.cloned.1.call-start = ((), (), s32[]{:S(2)}) async-start(), calls=%async_computation.13 | async-start | bytes 4718592 | tf_op jit(solution)/shard_map/psum | solution.py:180
  1156.7 176.6 %reduce-scatter.8.cloned.1.call-start = ((), (), s32[]{:S(2)}) async-start(), calls=%async_computation.18 | async-start | bytes 2654208 | tf_op jit(solution)/shard_map/reduce_scatter | solution.py:455
  1258.8 203.8 %reduce-scatter.6.cloned.1.call-start = ((), (), s32[]{:S(2)}) async-start(), calls=%async_computation.16 | async-start | bytes 7962624 | tf_op jit(solution)/shard_map/reduce_scatter | solution.py:452
  1280.1 532.1 %reduce-scatter.4.cloned.1.call-start = ((), (), s32[]{:S(2)}) async-start(), calls=%async_computation.14 | async-start | bytes 23887872 | tf_op jit(solution)/shard_map/reduce_scatter | solution.py:444
  1324.5 565.3 %all-reduce.33.cloned.1.call-start = ((), (), s32[]{:S(2)}) async-start(), calls=%async_computation.20 | async-start | bytes 1437696 | tf_op jit(solution)/shard_map/psum | solution.py:459
  1333.3 574.5 %all-gather.19.cloned.1.call-start = ((), (), s32[]{:S(2)}) async-start(), calls=%async_computation.19 | async-start | bytes 1474560 | tf_op jit(solution)/shard_map/all_gather | solution.py:467
  1333.8 613.3 %all-gather.17.cloned.1.call-start = ((), (), s32[]{:S(2)}) async-start(), calls=%async_computation.17 | async-start | bytes 5898240 | tf_op jit(solution)/shard_map/all_gather | solution.py:464
  1465.8 574.6 %all-gather.15.cloned.1.call-start = ((), (), s32[]{:S(2)}) async-start(), calls=%async_computation.15 | async-start | bytes 17694720 | tf_op jit(solution)/shard_map/all_gather | solution.py:463
  2090.3 203.2 %copy-start.104 = (f32[1152]{0:T(1024)}, f32[1152]{0:T(1024)S(1)}, u32[]{:S(2)}) copy-start(f32[1152]{0:T(1024)S(1)} %multiply_add_fusion.8) | copy-start | bytes 13828
  (157 other events, 2795.7 us)
Sparse Core Ops, SparseCore 0:
  10.8 57.7 all-gather.20
  71.3 106.8 all-gather.10
  180.3 321.8 all-gather.8
  504.8 59.9 all-gather.12
  567.6 54.3 all-reduce.16
  650.0 72.0 all-reduce.18
  737.9 55.7 all-reduce.20
  808.2 55.7 all-reduce.22
  906.6 55.7 all-reduce.24
  990.1 55.7 all-reduce.26
  1076.2 55.7 all-reduce.28
  1156.8 55.7 all-reduce.30
  1258.9 71.1 reduce-scatter.7
  1334.2 128.3 reduce-scatter.5
  1466.3 345.8 reduce-scatter.3
  1816.1 73.5 all-reduce.32
  1891.1 16.5 all-gather.18
  1909.7 37.4 all-gather.16
  1949.3 91.0 all-gather.14
where the time goes:
time: 2320 us; the launch traced here: 2310 us
  waiting for transfers between devices  1460 us (63%)
  local copies, waits for them, and re-layouts  348 us (15%)
  other arithmetic  193 us (8%)
  blocking collectives  140 us (6%)
  matrix products  139 us (6%)
    reduce_scatter x1, waiting for transfers between devices, shards(): lax.psum_scatter(jnp.concatenate([grad_in_head, grad_time, grad_temb_part...  346 us
    all_gather x1, waiting for transfers between devices, shards(): lax.all_gather(in_cols, 'dp', axis=1, tiled=True)  302 us
    psum x4, waiting for transfers between devices, input_sum(): return lax.psum(pieces, 'mp')  210 us
    unnamed x361, local copies, waits for them, and re-layouts  195 us
    psum x4, waiting for transfers between devices, branch_sum(): return lax.psum(pieces, 'mp')  148 us
    reduce_scatter x1, waiting for transfers between devices, shards(): lax.psum_scatter(grad_out_all.astype(jnp.bfloat16), 'dp', scatter_dimensi...  129 us
    dot_general x56, matrix products, contract(): return jnp.einsum(form, left, right, preferred_element_type=jnp.float32)  128 us
    all_gather x1, waiting for transfers between devices, shards(): lax.all_gather(out_cols, 'dp', axis=1, tiled=True)  107 us
  transfers between devices with their start and end apart: 19, of which 18 were waited for; matrix products, arithmetic and copies ran while one was open for 12% of the time, Pallas kernels for 0%

commit v1 on v0

v1 whole, which is shorter than its diff:
```python
import math

import jax
import jax.numpy as jnp
from jax import lax
from jax.sharding import PartitionSpec as P

HEAD_DIM = 72
D = 1152
FREQ = 256
CAP_DIM = 4096
CAP_LEN = 120
FRAMES = 8
GRID_H = 4
GRID_W = 8
PATCHES = 32
SLOTS = 2
STEP = 20
TOK_DEV = 512
CAP_PAD = 128


norm_eps = 1e-06
relative_rate = 0.5
tanh_coeff = math.sqrt(2.0 / math.pi)
angle_unit = math.pi / 2.0 / 1.008 / 1000.0


def product(left, right):
    return jnp.dot(left, right, preferred_element_type=jnp.float32)


def contract(form, left, right):
    return jnp.einsum(form, left, right, preferred_element_type=jnp.float32)


def gelu_tanh(values):
    return (
        0.5 * values * (1.0 + jnp.tanh(tanh_coeff * (values + 0.044715 * values * values * values)))
    )


def layer_norm(values):
    center = values - jnp.mean(values, axis=-1, keepdims=True)
    return center * lax.rsqrt(jnp.mean(center * center, axis=-1, keepdims=True) + norm_eps)


def modulate(hidden, shift_rows, scale_rows):
    return layer_norm(hidden) * (1.0 + scale_rows) + shift_rows


def modulate_grad(hidden, shift_rows, scale_rows, grad_rows):
    pullback = jax.vjp(modulate, hidden, shift_rows, scale_rows)[1]
    return pullback(grad_rows)


def act_grad(function, values, grad_rows):
    return jax.vjp(function, values)[1](grad_rows)[0]


def sincos(positions, table_width):
    half_width = table_width // 2
    frequency = jnp.exp(
        -math.log(10000.0) * jnp.arange(half_width).astype(jnp.float32) / half_width
    )
    angles = positions[:, None] * frequency[None, :]
    return jnp.concatenate([jnp.sin(angles), jnp.cos(angles)], axis=1)


def position_tables():
    patch_index = jnp.arange(GRID_H * GRID_W)
    spatial = jnp.concatenate(
        [
            sincos((patch_index // GRID_W).astype(jnp.float32), D // 2),
            sincos((patch_index % GRID_W).astype(jnp.float32), D // 2),
        ],
        axis=1,
    )
    temporal = sincos(jnp.arange(FRAMES).astype(jnp.float32), D)
    return (spatial, temporal)


def time_features(timesteps):
    half_width = FREQ // 2
    frequency = jnp.exp(
        -math.log(10000.0) * jnp.arange(half_width).astype(jnp.float32) / half_width
    )
    angles = timesteps.astype(jnp.float32)[:, None] * frequency[None, :]
    return jnp.concatenate([jnp.cos(angles), jnp.sin(angles)], axis=1)


def plan(timesteps):
    moment = timesteps.astype(jnp.float32)
    start_angle = 8.0 * angle_unit
    cos_start = math.cos(start_angle) ** 2
    remain_now = jnp.sin((1000.0 - moment) * angle_unit)
    remain_before = jnp.sin((1001.0 - moment) * angle_unit)
    alpha_now = remain_now * remain_now / cos_start
    alpha_before = remain_before * remain_before / cos_start
    rest_now = (
        jnp.sin(2.0 * start_angle + moment * angle_unit) * jnp.sin(moment * angle_unit) / cos_start
    )
    rest_before = (
        jnp.sin(2.0 * start_angle + (moment - 1.0) * angle_unit)
        * jnp.sin((moment - 1.0) * angle_unit)
        / cos_start
    )
    beta_now = (
        jnp.sin(2.0 * start_angle + (2.0 * moment - 1.0) * angle_unit)
        * math.sin(angle_unit)
        / (remain_before * remain_before)
    )
    posterior = beta_now * rest_before / rest_now
    kappa = beta_now * beta_now * alpha_before / (rest_now * alpha_now)
    return (alpha_now, rest_now, beta_now, posterior, kappa)


def patch_terms(output, target, squared, beta_rows, posterior_rows, kappa_rows):
    error_rows = output[:, :, 0:4] - target
    log_beta = jnp.log(beta_rows)[:, None, None]
    log_post = jnp.log(posterior_rows)[:, None, None]
    fraction = (output[:, :, 4:8] + 1.0) * 0.5
    log_model = fraction * log_beta + (1.0 - fraction) * log_post
    diverge = 0.5 * (
        -1.0
        + log_model
        - log_post
        + jnp.exp(log_post - log_model)
        + kappa_rows[:, None, None] * squared * jnp.exp(-log_model)
    )
    return jnp.mean(error_rows * error_rows, axis=(1, 2)) + jnp.mean(
        diverge, axis=(1, 2)
    ) / math.log(2.0)


def to_frames(stacked, head_count):
    leading = stacked.shape[0]
    return (
        stacked.reshape(leading, SLOTS, FRAMES, PATCHES, head_count, HEAD_DIM)
        .transpose(0, 1, 3, 2, 4, 5)
        .reshape(leading, SLOTS * PATCHES, FRAMES, head_count, HEAD_DIM)
    )


def from_frames(stacked, head_count):
    leading = stacked.shape[0]
    return (
        stacked.reshape(leading, SLOTS, PATCHES, FRAMES, head_count, HEAD_DIM)
        .transpose(0, 1, 3, 2, 4, 5)
        .reshape(leading, SLOTS * FRAMES * PATCHES, head_count * HEAD_DIM)
    )


def attend_forward(queries, key_rows, value_rows):
    scores = contract("bqhc,bkhc->bhqk", queries, key_rows) * HEAD_DIM ** (-0.5)
    highest = jnp.max(scores, axis=-1, keepdims=True)
    shifted = jnp.exp(scores - highest)
    denominator = jnp.sum(shifted, axis=-1, keepdims=True)
    weights = (shifted / denominator).astype(jnp.bfloat16)
    return (contract("bhqk,bkhc->bqhc", weights, value_rows), highest + jnp.log(denominator))


def attend_backward(queries, key_rows, value_rows, logsum, grad_mixed):
    scores = contract("bqhc,bkhc->bhqk", queries, key_rows) * HEAD_DIM ** (-0.5)
    probability = jnp.exp(scores - logsum)
    grad_value = contract("bhqk,bqhc->bkhc", probability.astype(jnp.bfloat16), grad_mixed)
    grad_prob = contract("bqhc,bkhc->bhqk", grad_mixed, value_rows)
    grad_scores = (
        probability * (grad_prob - jnp.sum(probability * grad_prob, axis=-1, keepdims=True))
    ).astype(jnp.bfloat16)
    grad_query = contract("bhqk,bkhc->bqhc", grad_scores, key_rows) * HEAD_DIM ** (-0.5)
    grad_key = contract("bhqk,bqhc->bkhc", grad_scores, queries) * HEAD_DIM ** (-0.5)
    return (grad_query, grad_key, grad_value)


def new_stat(old_stat, sums, length, inverse_sq):
    rho = 1.0 - STEP ** (-0.8)
    return rho * old_stat + (1.0 - rho) * (sums * inverse_sq / length + 1e-30)


def ratio_terms(weight, grad, rows_new, cols_new):
    ratio = jnp.sum(grad * grad / (rows_new[:, :, None] * cols_new[:, None, :]), axis=(1, 2))
    return jnp.stack([jnp.sum(rows_new, axis=1), ratio, jnp.sum(weight * weight, axis=(1, 2))])


def apply_update(weight, grad, rows_new, cols_new, mean_rows, spread, weight_scale):
    second = rows_new[:, :, None] * cols_new[:, None, :] / mean_rows[:, None, None]
    update = grad * lax.rsqrt(second)
    clipped = update / jnp.maximum(1.0, spread)[:, None, None]
    new_weight = weight - relative_rate * weight_scale[:, None, None] * clipped
    return (new_weight, new_weight.astype(jnp.bfloat16), clipped)


def token_sum(pieces):
    return lax.psum_scatter(
        pieces.astype(jnp.bfloat16), "mp", scatter_dimension=0, tiled=True
    ).astype(jnp.float32)


def token_gather(rows):
    return lax.all_gather(rows, "mp", axis=0, tiled=True)


def pad_samples(rows):
    stacked = rows.reshape(SLOTS, CAP_LEN, rows.shape[1])
    padded = jnp.pad(stacked, ((0, 0), (0, CAP_PAD - CAP_LEN), (0, 0)))
    return padded.reshape(SLOTS * CAP_PAD, rows.shape[1])


def cut_samples(rows):
    stacked = rows.reshape(SLOTS, CAP_PAD, rows.shape[1])[:, 0:CAP_LEN]
    return stacked.reshape(SLOTS * CAP_LEN, rows.shape[1])


def side_by_side(stacked):
    return stacked.transpose(1, 0, 2).reshape(stacked.shape[1], -1)


def heads_of(rows, lead, count):
    return rows.reshape(*lead, count, HEAD_DIM)


def spatial_heads(rows, count):
    return rows.reshape(SLOTS * FRAMES, PATCHES, count, HEAD_DIM)


def temporal_heads(rows, count):
    return to_frames(rows[None], count)[0]


def shards(
    latents, gaussian_noise, timesteps, counts, captions,
    w_in, w_out, w_cap, w_small,
    rows_in, cols_in, rows_out, cols_out, rows_cap, cols_cap, rows_small, cols_small,
):
    bfloat = jnp.bfloat16
    mp_index = lax.axis_index("mp")
    dp_index = lax.axis_index("dp")
    mp_size = lax.axis_size("mp")
    dp_size = lax.axis_size("dp")
    local_width = w_in.shape[2] // mp_size
    head_count = local_width // HEAD_DIM
    col_start = mp_index * local_width
    row_count_own = w_in.shape[1]
    row_start = dp_index * row_count_own
    cap_rows_own = w_cap.shape[0]
    small_rows = 56 + FREQ
    per_sample = FRAMES * PATCHES
    own_tokens = TOK_DEV // mp_size
    token_start = mp_index * own_tokens
    sample = token_start // per_sample
    wide = 4 * local_width
    lw = local_width

    in_cols = lax.dynamic_slice_in_dim(w_in[0:13], col_start, lw, 2).astype(bfloat)
    out_cols = lax.dynamic_slice_in_dim(w_out, col_start, lw, 2).astype(bfloat)
    cap_cols = lax.dynamic_slice_in_dim(w_cap, col_start, lw, 1).astype(bfloat)
    pack_s = side_by_side(jnp.concatenate([in_cols[0:3], out_cols[0:1]], axis=0))
    pack_t = side_by_side(jnp.concatenate([in_cols[3:6], out_cols[1:2]], axis=0))
    pack_c = side_by_side(jnp.concatenate([in_cols[6:9], out_cols[2:3]], axis=0))
    pack_i = side_by_side(in_cols[9:13])
    pack_o = side_by_side(out_cols[3:7])
    pack_x = jnp.concatenate([cap_cols, out_cols[7]], axis=0)
    full_s = lax.all_gather(pack_s, "dp", axis=0, tiled=True)
    full_t = lax.all_gather(pack_t, "dp", axis=0, tiled=True)
    full_x = lax.all_gather(pack_x, "dp", axis=0, tiled=False)
    full_c = lax.all_gather(pack_c, "dp", axis=0, tiled=True)
    full_i = lax.all_gather(pack_i, "dp", axis=0, tiled=True)
    full_o = lax.all_gather(pack_o, "dp", axis=0, tiled=True)
    full_cap = full_x[:, 0:cap_rows_own].reshape(CAP_DIM, lw)
    full_c2 = full_x[:, cap_rows_own:].reshape(D, lw)
    mod_rows = w_in[13:19].astype(bfloat)
    temb_rows = w_in[19].astype(bfloat)

    full_small = w_small.astype(bfloat)
    patch_w = full_small[0:16]
    freq_w = full_small[16 : 16 + FREQ]
    tables = full_small[16 + FREQ : 24 + FREQ].astype(jnp.float32)
    final_w = full_small[24 + FREQ :]

    def own_rows(rows):
        return lax.dynamic_slice_in_dim(rows, token_start, own_tokens, 0)

    def own_cols(rows):
        return lax.dynamic_slice_in_dim(rows, row_start, row_count_own, 1)

    all_times = lax.all_gather(timesteps, "dp", axis=0, tiled=True)
    alpha_now, rest_now, beta_now, posterior, kappa = plan(timesteps)
    features = time_features(all_times).astype(bfloat)
    first_pre = product(features, freq_w)
    first_act = jax.nn.silu(first_pre).astype(bfloat)
    time_emb_all = lax.psum(product(own_cols(first_act), temb_rows), "dp")
    temb_act = jax.nn.silu(time_emb_all).astype(bfloat)
    mod_part = contract("sd,kde->ske", own_cols(temb_act), mod_rows)
    modulation = (
        lax.psum_scatter(mod_part, "dp", scatter_dimension=0, tiled=True) + tables[None, 0:6]
    )
    time_emb = lax.dynamic_slice_in_dim(time_emb_all, dp_index * SLOTS, SLOTS, 0)
    mods_own = lax.dynamic_index_in_dim(modulation, sample, 0, keepdims=False)
    shift_a, scale_a, gate_a, shift_b, scale_b, gate_b = [
        mods_own[number : number + 1] for number in range(6)
    ]
    temb_own = lax.dynamic_slice_in_dim(time_emb, sample, 1, 0)

    noisy_low = (
        jnp.sqrt(alpha_now)[:, None, None, None] * latents.astype(jnp.float32)
        + jnp.sqrt(rest_now)[:, None, None, None] * gaussian_noise
    ).astype(bfloat)
    patches = noisy_low.reshape(TOK_DEV, 16)
    spatial_pos, temporal_pos = position_tables()
    start_hidden = (
        product(patches, patch_w).reshape(SLOTS * FRAMES, PATCHES, D) + spatial_pos[None]
    ).reshape(SLOTS, per_sample, D)
    start_own = own_rows(start_hidden.reshape(TOK_DEV, D))

    cap_rows = captions.reshape(SLOTS * CAP_LEN, CAP_DIM)
    cap_mid = product(cap_rows, full_cap)
    cap_act = gelu_tanh(cap_mid).astype(bfloat)
    context_own = token_sum(pad_samples(contract("re,de->rd", cap_act, full_c2))).astype(bfloat)
    context_low = cut_samples(token_gather(context_own))

    normed_a = (
        modulate(start_hidden, modulation[:, 0][:, None], modulation[:, 1][:, None])
        .astype(bfloat)
        .reshape(TOK_DEV, D)
    )
    qkv = product(normed_a, full_s[:, 0 : 3 * lw]).astype(bfloat)
    qkv_s = [spatial_heads(qkv[:, k * lw : (k + 1) * lw], head_count) for k in range(3)]
    mixed_s, logsum_s = attend_forward(*qkv_s)
    mixed_s_low = mixed_s.astype(bfloat).reshape(TOK_DEV, lw)
    branch_s = token_sum(contract("te,de->td", mixed_s_low, full_s[:, 3 * lw :]))
    hidden_s = start_own + gate_a * branch_s
    frame_start = (token_start % per_sample) // PATCHES
    frames_own = own_tokens // PATCHES
    temporal_own = lax.dynamic_slice_in_dim(temporal_pos, frame_start, frames_own, 0)
    timed_own = (
        hidden_s.reshape(frames_own, PATCHES, D) + temporal_own[:, None, :]
    ).astype(bfloat)
    timed_low = token_gather(timed_own.reshape(own_tokens, D))
    qkv = product(timed_low, full_t[:, 0 : 3 * lw]).astype(bfloat)
    qkv_t = [temporal_heads(qkv[:, k * lw : (k + 1) * lw], head_count) for k in range(3)]
    mixed_t, logsum_t = attend_forward(*qkv_t)
    mixed_t_low = from_frames(mixed_t.astype(bfloat)[None], head_count)[0]
    branch_t = token_sum(contract("te,de->td", mixed_t_low, full_t[:, 3 * lw :]))
    hidden_t = hidden_s + gate_a * branch_t
    hidden_low = token_gather(hidden_t.astype(bfloat))
    query_c = (
        product(hidden_low, full_c[:, 0:lw])
        .astype(bfloat)
        .reshape(SLOTS, per_sample, head_count, HEAD_DIM)
    )
    key_value = product(context_low, full_c[:, lw : 3 * lw]).astype(bfloat)
    key_c = key_value[:, 0:lw].reshape(SLOTS, CAP_LEN, head_count, HEAD_DIM)
    value_c = key_value[:, lw:].reshape(SLOTS, CAP_LEN, head_count, HEAD_DIM)
    mixed_c, logsum_c = attend_forward(query_c, key_c, value_c)
    mixed_c_low = mixed_c.astype(bfloat).reshape(TOK_DEV, lw)
    hidden_c = hidden_t + token_sum(contract("te,de->td", mixed_c_low, full_c[:, 3 * lw :]))
    normed_b = token_gather(modulate(hidden_c, shift_b, scale_b).astype(bfloat))
    inner_pre = product(normed_b, full_i)
    inner_act = gelu_tanh(inner_pre).astype(bfloat)
    branch_m = token_sum(contract("te,de->td", inner_act, full_o))
    hidden_m = hidden_c + gate_b * branch_m
    shift_f = tables[6:7] + temb_own
    scale_f = tables[7:8] + temb_own
    normed_f = modulate(hidden_m, shift_f, scale_f).astype(bfloat)
    output = contract("td,od->to", normed_f, final_w).reshape(own_tokens, 4, 8)
    target = own_rows(gaussian_noise.reshape(TOK_DEV, 4, 4))
    error_rows = output[:, :, 0:4] - target
    squared = error_rows * error_rows
    live = (sample * per_sample < counts[0]).astype(jnp.float32)

    def of_sample(values):
        return jnp.broadcast_to(lax.dynamic_slice_in_dim(values, sample, 1, 0), (own_tokens,))

    beta_rows = of_sample(beta_now)
    posterior_rows = of_sample(posterior)
    kappa_rows = of_sample(kappa)

    def patch_loss(values):
        return jnp.sum(
            patch_terms(values, target, squared, beta_rows, posterior_rows, kappa_rows) * live
        )

    loss_local, loss_pull = jax.vjp(patch_loss, output)
    grad_output = loss_pull(jnp.ones_like(loss_local))[0].astype(bfloat).reshape(own_tokens, 32)
    grad_final = contract("to,td->od", grad_output, normed_f)
    grad_normed = contract("to,od->td", grad_output, final_w)
    grad_hidden, grad_shift_f, grad_scale_f = modulate_grad(hidden_m, shift_f, scale_f, grad_normed)
    grad_gate_b = jnp.sum(grad_hidden * branch_m, axis=0, keepdims=True)
    grad_branch = token_gather((gate_b * grad_hidden).astype(bfloat))
    grad_inner = act_grad(gelu_tanh, inner_pre, product(grad_branch, full_o)).astype(bfloat)
    part = contract("te,de->td", grad_inner, full_i)
    grad_pack_o = contract("td,te->de", grad_branch, inner_act)
    grad_pack_i = contract("td,te->de", normed_b, grad_inner)

    def row_sum(pieces):
        return lax.psum_scatter(
            pieces.astype(bfloat), "dp", scatter_dimension=0, tiled=True
        )

    sum_o = row_sum(grad_pack_o)
    sum_i = row_sum(grad_pack_i)
    grad_normed = token_sum(part)
    grad_more, grad_shift_b, grad_scale_b = modulate_grad(hidden_c, shift_b, scale_b, grad_normed)
    grad_hidden = grad_hidden + grad_more
    grad_branch = token_gather(grad_hidden.astype(bfloat))
    grad_mixed = (
        product(grad_branch, full_c[:, 3 * lw :])
        .astype(bfloat)
        .reshape(SLOTS, per_sample, head_count, HEAD_DIM)
    )
    grad_query, grad_key, grad_value = attend_backward(
        query_c, key_c, value_c, logsum_c, grad_mixed
    )
    grad_query = grad_query.astype(bfloat).reshape(TOK_DEV, lw)
    grad_kv = jnp.concatenate(
        [
            grad_key.astype(bfloat).reshape(SLOTS * CAP_LEN, lw),
            grad_value.astype(bfloat).reshape(SLOTS * CAP_LEN, lw),
        ],
        axis=1,
    )
    part = contract("te,de->td", grad_query, full_c[:, 0:lw])
    part_context = contract("re,de->rd", grad_kv, full_c[:, lw : 3 * lw])
    sum_c = row_sum(
        jnp.concatenate(
            [
                contract("td,te->de", hidden_low, grad_query),
                contract("rd,re->de", context_low, grad_kv),
                contract("td,te->de", grad_branch, mixed_c_low),
            ],
            axis=1,
        )
    )
    grad_hidden = grad_hidden + token_sum(part)
    grad_gate_a = jnp.sum(grad_hidden * branch_t, axis=0, keepdims=True)
    grad_branch = token_gather((gate_a * grad_hidden).astype(bfloat))
    grad_mixed = temporal_heads(
        product(grad_branch, full_t[:, 3 * lw :]).astype(bfloat), head_count
    )
    grads_t = attend_backward(*qkv_t, logsum_t, grad_mixed)
    grad_qkv = from_frames(jnp.stack(grads_t).astype(bfloat), head_count)
    grad_qkv = jnp.concatenate([grad_qkv[0], grad_qkv[1], grad_qkv[2]], axis=1)
    part = contract("te,de->td", grad_qkv, full_t[:, 0 : 3 * lw])
    sum_t = row_sum(
        jnp.concatenate(
            [
                contract("td,te->de", timed_low, grad_qkv),
                contract("td,te->de", grad_branch, mixed_t_low),
            ],
            axis=1,
        )
    )
    grad_hidden = grad_hidden + token_sum(part)
    grad_gate_a = grad_gate_a + jnp.sum(grad_hidden * branch_s, axis=0, keepdims=True)
    grad_branch = token_gather((gate_a * grad_hidden).astype(bfloat))
    grad_mixed = spatial_heads(
        product(grad_branch, full_s[:, 3 * lw :]).astype(bfloat), head_count
    )
    grads_s = attend_backward(*qkv_s, logsum_s, grad_mixed)
    grad_qkv = jnp.concatenate(
        [grad.astype(bfloat).reshape(TOK_DEV, lw) for grad in grads_s], axis=1
    )
    part = contract("te,de->td", grad_qkv, full_s[:, 0 : 3 * lw])
    sum_s = row_sum(
        jnp.concatenate(
            [
                contract("td,te->de", normed_a, grad_qkv),
                contract("td,te->de", grad_branch, mixed_s_low),
            ],
            axis=1,
        )
    )
    grad_context = cut_samples(
        token_gather(token_sum(pad_samples(part_context)).astype(bfloat))
    )
    grad_cap2 = contract("rd,re->de", grad_context, cap_act)
    grad_cap_mid = act_grad(
        gelu_tanh, cap_mid, contract("rd,de->re", grad_context, full_c2)
    ).astype(bfloat)
    grad_cap = contract("rc,re->ce", cap_rows, grad_cap_mid)
    sum_x = row_sum(
        jnp.concatenate(
            [
                grad_cap.reshape(dp_size, cap_rows_own, lw),
                grad_cap2.reshape(dp_size, row_count_own, lw),
            ],
            axis=1,
        ).reshape(dp_size * (cap_rows_own + row_count_own), lw)
    )
    grad_normed = token_sum(part)
    grad_more, grad_shift_a, grad_scale_a = modulate_grad(start_own, shift_a, scale_a, grad_normed)
    grad_hidden = grad_hidden + grad_more
    grad_patch = contract("ti,td->id", own_rows(patches), grad_hidden.astype(bfloat))
    grad_mods = jnp.concatenate(
        [
            grad_shift_a, grad_scale_a, grad_gate_a, grad_shift_b, grad_scale_b, grad_gate_b,
            grad_shift_f, grad_scale_f,
        ],
        axis=0,
    )
    placed = jnp.where(
        (jnp.arange(SLOTS) == sample)[:, None, None], grad_mods[None], 0.0
    )
    grad_mods = lax.psum(placed, "mp")
    mods_all = lax.all_gather(grad_mods.astype(bfloat), "dp", axis=0, tiled=True)
    grad_mods_low = mods_all[:, 0:6]
    grad_tables = jnp.sum(mods_all.astype(jnp.float32), axis=0)
    grad_temb_act = contract("ske,kde->sd", grad_mods_low, mod_rows)
    grad_temb = act_grad(jax.nn.silu, own_cols(time_emb_all), grad_temb_act) + own_cols(
        (mods_all[:, 6].astype(jnp.float32) + mods_all[:, 7].astype(jnp.float32))
    )
    grad_temb_low = lax.all_gather(grad_temb.astype(bfloat), "dp", axis=1, tiled=True)
    grad_first_own = act_grad(
        jax.nn.silu, own_cols(first_pre), contract("sd,id->si", grad_temb_low, temb_rows)
    ).astype(bfloat)
    grad_first = lax.all_gather(grad_first_own, "dp", axis=1, tiled=True)
    grad_time = contract("sd,ske->kde", own_cols(temb_act), grad_mods_low)
    grad_temb_part = contract("si,sd->id", own_cols(first_act), grad_temb_low)
    grad_freq = contract("sf,sd->fd", features, grad_first)
    small_part = lax.psum(jnp.concatenate([grad_patch, grad_final], axis=0), ("dp", "mp"))
    sum_small = jnp.concatenate([small_part[0:16], grad_freq, grad_tables, small_part[16:]], axis=0)

    def all_columns(rows):
        blocks = lax.all_gather(rows, "mp", axis=0, tiled=False)
        kinds = rows.shape[1] // lw
        stacked = blocks.reshape(mp_size, rows.shape[0], kinds, lw)
        return stacked.transpose(2, 1, 0, 3).reshape(kinds, rows.shape[0], mp_size * lw)

    whole_s, whole_t, whole_c, whole_i, whole_o, whole_x = [
        all_columns(rows).astype(jnp.float32)
        for rows in (sum_s, sum_t, sum_c, sum_i, sum_o, sum_x)
    ]
    sum_in = jnp.concatenate(
        [whole_s[0:3], whole_t[0:3], whole_c[0:3], whole_i, grad_time, grad_temb_part[None]], axis=0
    )
    sum_out = jnp.concatenate(
        [whole_s[3:4], whole_t[3:4], whole_c[3:4], whole_o, whole_x[:, cap_rows_own:]], axis=0
    )
    sum_cap = whole_x[0, 0:cap_rows_own]
    count_local = counts[0].astype(jnp.float32)
    square_in = sum_in * sum_in
    square_out = sum_out * sum_out
    square_cap = sum_cap * sum_cap
    square_small = sum_small * sum_small
    row_in_total = jnp.sum(square_in, axis=2)
    row_out_total = jnp.sum(square_out, axis=2)
    row_cap_total = jnp.sum(square_cap, axis=1)
    row_small_total = jnp.sum(square_small, axis=1)
    col_small_total = jnp.sum(square_small, axis=0)
    col_in_total, col_out_total, col_cap_total, loss_total, count_total = (
        lax.psum(jnp.sum(square_in, axis=1).astype(jnp.bfloat16), "dp").astype(jnp.float32),
        lax.psum(jnp.sum(square_out, axis=1).astype(jnp.bfloat16), "dp").astype(jnp.float32),
        lax.psum(jnp.sum(square_cap, axis=0).astype(jnp.bfloat16), "dp").astype(jnp.float32),
        lax.psum(loss_local, ("dp", "mp")),
        lax.psum(count_local, "dp"),
    )
    inverse = 1.0 / count_total
    inverse_sq = inverse * inverse
    rows_in_new = new_stat(rows_in, row_in_total, D, inverse_sq)
    cols_in_new = new_stat(cols_in, col_in_total, D, inverse_sq)
    rows_out_new = new_stat(rows_out, row_out_total, D, inverse_sq)
    cols_out_new = new_stat(cols_out, col_out_total, D, inverse_sq)
    rows_cap_new = new_stat(rows_cap, row_cap_total, D, inverse_sq)
    cols_cap_new = new_stat(cols_cap, col_cap_total, CAP_DIM, inverse_sq)
    rows_small_new = new_stat(rows_small, row_small_total, D, inverse_sq)
    cols_small_new = new_stat(cols_small, col_small_total, small_rows, inverse_sq)
    grad_in = sum_in * inverse
    grad_out = sum_out * inverse
    grad_cap_all = (sum_cap * inverse)[None]
    grad_small_all = (sum_small * inverse)[None]
    ratios = lax.psum(
        jnp.concatenate(
            [
                ratio_terms(w_in, grad_in, rows_in_new, cols_in_new),
                ratio_terms(w_out, grad_out, rows_out_new, cols_out_new),
                ratio_terms(w_cap[None], grad_cap_all, rows_cap_new[None], cols_cap_new[None]),
            ],
            axis=1,
        ),
        "dp",
    )
    totals = jnp.concatenate(
        [
            ratios,
            ratio_terms(w_small[None], grad_small_all, rows_small_new[None], cols_small_new[None]),
        ],
        axis=1,
    )
    row_count = jnp.array([float(D)] * 28 + [float(CAP_DIM), float(small_rows)], jnp.float32)
    mean_rows = totals[0] / row_count
    spreads = jnp.sqrt(mean_rows * totals[1] / (row_count * D))
    weight_scale = jnp.sqrt(totals[2] / (row_count * D))
    in_new, in_copy, in_update = apply_update(
        w_in, grad_in, rows_in_new, cols_in_new, mean_rows[0:20], spreads[0:20], weight_scale[0:20]
    )
    out_new, out_copy, out_update = apply_update(
        w_out,
        grad_out,
        rows_out_new,
        cols_out_new,
        mean_rows[20:28],
        spreads[20:28],
        weight_scale[20:28],
    )
    cap_new, cap_copy, cap_update = apply_update(
        w_cap[None],
        grad_cap_all,
        rows_cap_new[None],
        cols_cap_new[None],
        mean_rows[28:29],
        spreads[28:29],
        weight_scale[28:29],
    )
    small_new, small_copy, small_update = apply_update(
        w_small[None],
        grad_small_all,
        rows_small_new[None],
        cols_small_new[None],
        mean_rows[29:30],
        spreads[29:30],
        weight_scale[29:30],
    )
    return (
        loss_total * inverse,
        in_new,
        in_copy,
        in_update,
        rows_in_new,
        cols_in_new,
        out_new,
        out_copy,
        out_update,
        rows_out_new,
        cols_out_new,
        cap_new[0],
        cap_copy[0],
        cap_update[0],
        rows_cap_new,
        cols_cap_new,
        small_new[0],
        small_copy[0],
        small_update[0],
        rows_small_new,
        cols_small_new,
        spreads,
    )


def solution(mesh):
    in_specs = (
        P("dp", None, None, None),
        P("dp", None, None, None),
        P("dp"),
        P("dp"),
        P("dp", None, None),
        P(None, "dp", None),
        P(None, "dp", None),
        P("dp", None),
        P(),
        P(None, "dp"),
        P(),
        P(None, "dp"),
        P(),
        P("dp"),
        P(),
        P(),
        P(),
    )
    out_specs = (
        P(),
        P(None, "dp", None),
        P(None, "dp", None),
        P(None, "dp", None),
        P(None, "dp"),
        P(),
        P(None, "dp", None),
        P(None, "dp", None),
        P(None, "dp", None),
        P(None, "dp"),
        P(),
        P("dp", None),
        P("dp", None),
        P("dp", None),
        P("dp"),
        P(),
        P(),
        P(),
        P(),
        P(),
        P(),
        P(),
    )
    return jax.shard_map(shards, mesh=mesh, in_specs=in_specs, out_specs=out_specs, check_vma=False)
```

time: 2320 us -> 1950 us (0.84)
  waiting for transfers between devices: 1460 us -> 1180 us
  local copies, waits for them, and re-layouts: 348 us -> 240 us
  blocking collectives: 140 us -> 212 us
  other arithmetic: 193 us -> 151 us
    all_gather x7 -> x19, waiting for transfers between devices: 611 us -> 440 us  [the longest x7 100 us: token_gather(): return lax.all_gather(rows, 'mp', axis=0, tiled=True)]
    psum x9 -> x3, waiting for transfers between devices: 375 us -> 219 us  [the longest x1 92.9 us: shards(): lax.psum(jnp.concatenate([grad_patch, grad_final], axis=0), ('dp', 'mp'))]
    unnamed x19 -> x41, waiting for transfers between devices: 0.8 us -> 131 us
    unnamed x361 -> x331, local copies, waits for them, and re-layouts: 195 us -> 71.3 us
    all_gather x1 -> x5, blocking collectives: 10.9 us -> 108 us  [the longest x1 32.4 us: shards(): lax.all_gather(grad_mods.astype(bfloat), 'dp', axis=0, tiled=True)]
    reduce_scatter x3 -> x15, waiting for transfers between devices: 475 us -> 390 us  [the longest x5 225 us: row_sum(): lax.psum_scatter(pieces.astype(bfloat), 'dp', scatter_dimension=0, tiled=...]
    psum x3, blocking collectives: 111 us -> 69.6 us  [the longest x1 37.6 us: shards(): lax.psum(loss_local, ('dp', 'mp'))]
    convert_element_type x8 -> x21, local copies, waits for them, and re-layouts: 12.6 us -> 54.1 us  [the longest x9 47.8 us: shards(): all_columns(rows).astype(jnp.float32)]
  transfers between devices with their start and end apart: 19 -> 39, of which waited for: 18 -> 33; matrix products, arithmetic and copies ran while one was open for 12% -> 15% of each run, Pallas kernels for 0% -> 0%
where the time goes in v1:
time: 1950 us; the launch traced here: 1940 us
  waiting for transfers between devices  1180 us (61%)
  local copies, waits for them, and re-layouts  240 us (12%)
  blocking collectives  212 us (11%)
  other arithmetic  151 us (8%)
  matrix products  132 us (7%)
  between operations  26.1 us (1%)
    reduce_scatter x5, waiting for transfers between devices, row_sum(): lax.psum_scatter(pieces.astype(bfloat), 'dp', scatter_dimension=0, tiled=...  225 us
    reduce_scatter x10, waiting for transfers between devices, token_sum(): lax.psum_scatter(pieces.astype(jnp.bfloat16), 'mp', scatter_dimension=0,...  165 us
    unnamed x41, waiting for transfers between devices  131 us
    all_gather x7, waiting for transfers between devices, token_gather(): return lax.all_gather(rows, 'mp', axis=0, tiled=True)  100 us
    dot_general x49, matrix products, contract(): return jnp.einsum(form, left, right, preferred_element_type=jnp.float32)  93.3 us
    psum x1, waiting for transfers between devices, shards(): lax.psum(jnp.concatenate([grad_patch, grad_final], axis=0), ('dp', 'mp'))  92.9 us
    unnamed x331, local copies, waits for them, and re-layouts  71.3 us
    psum x1, waiting for transfers between devices, shards(): lax.psum(jnp.sum(square_cap, axis=0).astype(jnp.bfloat16), 'dp')  70.2 us
  transfers between devices with their start and end apart: 39, of which 33 were waited for; matrix products, arithmetic and copies ran while one was open for 15% of the time, Pallas kernels for 0%

profile of v1, /device:TPU:0, one launch (start us, length us, event | category | flops | bytes accessed | tf_op | source)
XLA Modules:
  0.0 1943.5 jit_solution(11776092491211616070)
XLA Ops:
  52.6 56.3 %all-reduce.12.cloned.1.call-done = f32[16,1152]{1,0:T(8,128)} async-done(((f32[16,1152]{1,0:T(8,128)}), f32[16,1152]{1,0:T(8,128)}) %all-reduce.12.cloned.1.call-update) | async-done | bytes 73744 | tf_op jit(solution)/shard_map/psum | solution.py:292
  131.7 53.4 %all-reduce.16.cloned.1.call-done = f32[16,6,1152]{2,0,1:T(8,128)} async-done(((f32[16,6,1152]{2,0,1:T(8,128)}), f32[16,6,1152]{2,0,1:T(8,128)}) %all-reduce.16.cloned.1.call-update) | async-done | bytes 442384
  189.0 52.9 %all-gather.31.cloned.1.call-done = bf16[1152,1152]{1,0:T(8,128)(2,1)} async-done(((bf16[144,1152]{1,0:T(8,128)(2,1)}), bf16[1152,1152]{1,0:T(8,128)(2,1)}) %all-gather.31.cloned.1.call-update) | async-done | bytes 2654224 | tf_op jit(solution)/shard_map/all_gather | solution.py:264
  288.7 50.1 %all-gather.35.cloned.1.call-done = bf16[1152,1152]{1,0:T(8,128)(2,1)} async-done(((bf16[144,1152]{1,0:T(8,128)(2,1)}), bf16[1152,1152]{1,0:T(8,128)(2,1)}) %all-gather.35.cloned.1.call-update) | async-done | bytes 2654224 | tf_op jit(solution)/shard_map/all_gather | solution.py:265
  374.3 49.8 %all-gather.65.cloned.1.call-done = bf16[8,656,288]{1,2,0:T(8,128)(2,1)} async-done(((bf16[1,656,288]{1,2,0:T(8,128)(2,1)}), bf16[8,656,288]{1,2,0:T(8,128)(2,1)}) %all-gather.65.cloned.1.call-update) | async-done | bytes 3022864 | tf_op jit(solution)/shard_map/all_gather | solution.py:266
  453.7 23.1 %reduce-scatter.30.cloned.1.call-done = bf16[64,1152]{1,0:T(8,128)(2,1)} async-done(((bf16[256,1152]{1,0:T(8,128)(2,1)}), bf16[64,1152]{1,0:T(8,128)(2,1)}) %reduce-scatter.30.cloned.1.call-update) | async-done | bytes 147472 | tf_op jit(solution)/shard_map/reduce_scatter | solution.py:195
  484.2 49.6 %all-gather.37.cloned.1.call-done = bf16[1152,1152]{1,0:T(8,128)(2,1)} async-done(((bf16[144,1152]{1,0:T(8,128)(2,1)}), bf16[1152,1152]{1,0:T(8,128)(2,1)}) %all-gather.37.cloned.1.call-update) | async-done | bytes 2654224 | tf_op jit(solution)/shard_map/all_gather | solution.py:267
  564.0 23.3 %reduce-scatter.32.cloned.1.call-done = bf16[128,1152]{1,0:T(8,128)(2,1)} async-done(((bf16[512,1152]{1,0:T(8,128)(2,1)}), bf16[128,1152]{1,0:T(8,128)(2,1)}) %reduce-scatter.32.cloned.1.call-update) | async-done | bytes 294928 | tf_op jit(solution)/shard_map/reduce_scatter | solution.py:195
  596.4 48.0 %all-gather.43.cloned.1.call-done = bf16[1152,1152]{1,0:T(8,128)(2,1)} async-done(((bf16[144,1152]{1,0:T(8,128)(2,1)}), bf16[1152,1152]{1,0:T(8,128)(2,1)}) %all-gather.43.cloned.1.call-update) | async-done | bytes 2654224 | tf_op jit(solution)/shard_map/all_gather | solution.py:268
  667.3 52.2 %all-gather.45.cloned.1.call-done = bf16[1152,1152]{1,0:T(8,128)(2,1)} async-done(((bf16[144,1152]{1,0:T(8,128)(2,1)}), bf16[1152,1152]{1,0:T(8,128)(2,1)}) %all-gather.45.cloned.1.call-update) | async-done | bytes 2654224 | tf_op jit(solution)/shard_map/all_gather | solution.py:269
  787.4 25.7 %reduce-scatter.36.cloned.1.call-done = bf16[128,1152]{1,0:T(8,128)(2,1)} async-done(((bf16[512,1152]{1,0:T(8,128)(2,1)}), bf16[128,1152]{1,0:T(8,128)(2,1)}) %reduce-scatter.36.cloned.1.call-update) | async-done | bytes 294928 | tf_op jit(solution)/shard_map/reduce_scatter | solution.py:195
  847.2 25.7 %reduce-scatter.38.cloned.1.call-done = bf16[128,1152]{1,0:T(8,128)(2,1)} async-done(((bf16[512,1152]{1,0:T(8,128)(2,1)}), bf16[128,1152]{1,0:T(8,128)(2,1)}) %reduce-scatter.38.cloned.1.call-update) | async-done | bytes 294928 | tf_op jit(solution)/shard_map/reduce_scatter | solution.py:195
  1008.1 50.2 %reduce-scatter.46.cloned.1.call-done = bf16[144,1152]{1,0:T(8,128)(2,1)} async-done(((bf16[1152,1152]{1,0:T(8,128)(2,1)}), bf16[144,1152]{1,0:T(8,128)(2,1)}) %reduce-scatter.46.cloned.1.call-update) | async-done | bytes 331792 | tf_op jit(solution)/shard_map/reduce_scatter | solution.py:397
  1058.4 74.1 %reduce-scatter.42.cloned.1.call-done = bf16[144,1152]{1,0:T(8,128)(2,1)} async-done(((bf16[1152,1152]{1,0:T(8,128)(2,1)}), bf16[144,1152]{1,0:T(8,128)(2,1)}) %reduce-scatter.42.cloned.1.call-update) | async-done | bytes 331792 | tf_op jit(solution)/shard_map/reduce_scatter | solution.py:397
  1132.6 74.3 %reduce-scatter.54.cloned.1.call-done = bf16[144,1152]{1,0:T(8,128)(2,1)} async-done(((bf16[1152,1152]{1,0:T(8,128)(2,1)}), bf16[144,1152]{1,0:T(8,128)(2,1)}) %reduce-scatter.54.cloned.1.call-update) | async-done | bytes 331792 | tf_op jit(solution)/shard_map/reduce_scatter | solution.py:397
  1218.8 76.6 %reduce-scatter.56.cloned.1.call-done = bf16[656,288]{1,0:T(8,128)(2,1)} async-done(((bf16[5248,288]{1,0:T(8,128)(2,1)}), bf16[656,288]{1,0:T(8,128)(2,1)}) %reduce-scatter.56.cloned.1.call-update) | async-done | bytes 377872
  1343.4 37.6 %psum.64 = f32[]{:T(128)} all-reduce(f32[]{:T(128)} %multiply_reduce_fusion.21), channel_id=1, replica_groups=mesh['dp'=8,'mp'=4] {'dp','mp'}, use_global_device_ids=true, to_apply=%region_22.23 | all-reduce | flops 1 | bytes 8 | tf_op jit(solution)/shard_map/psum | solution.py:555
  1432.8 26.4 %reduce-scatter.52.cloned.1.call-done = bf16[144,1152]{1,0:T(8,128)(2,1)} async-done(((bf16[1152,1152]{1,0:T(8,128)(2,1)}), bf16[144,1152]{1,0:T(8,128)(2,1)}) %reduce-scatter.52.cloned.1.call-update) | async-done | bytes 331792 | tf_op jit(solution)/shard_map/reduce_scatter | solution.py:397
  1459.4 21.8 %all-gather.67.cloned.1.call-done = bf16[4,656,288]{1,2,0:T(8,128)(2,1)} async-done(((bf16[1,656,288]{1,2,0:T(8,128)(2,1)}), bf16[4,656,288]{1,2,0:T(8,128)(2,1)}) %all-gather.67.cloned.1.call-update) | async-done | bytes 1511440 | tf_op jit(solution)/shard_map/all_gather | solution.py:525
  1496.5 32.4 %all_gather.120 = bf16[16,8,1152]{2,1,0:T(8,128)(2,1)S(1)} all-gather(bf16[2,8,1152]{2,1,0:T(8,128)(2,1)S(1)} %psum.66), channel_id=1, replica_groups=mesh['dp'=8,'mp'=4] {'dp'}, dimensions={0}, use_global_device_ids=true | all-gather | bytes 331776 | tf_op jit(solution)/shard_map/all_gather | solution.py:506
  1531.4 30.9 %all-gather.8 = bf16[8,144,16]{1,2,0:T(8,128)(2,1)S(1)} all-gather(bf16[1,144,16]{1,2,0:T(8,128)(2,1)S(1)} %fusion.164), channel_id=1, replica_groups=mesh['dp'=8,'mp'=4] {'dp'}, dimensions={0}, use_global_device_ids=true | all-gather | bytes 41472 | tf_op jit(solution)/shard_map/all_gather | solution.py:513
  1563.7 30.6 %all-gather.10 = bf16[8,144,16]{1,2,0:T(8,128)(2,1)S(1)} all-gather(bf16[1,144,16]{1,2,0:T(8,128)(2,1)S(1)} %fusion.159), channel_id=1, replica_groups=mesh['dp'=8,'mp'=4] {'dp'}, dimensions={0}, use_global_device_ids=true | all-gather | bytes 41472 | tf_op jit(solution)/shard_map/all_gather | solution.py:517
  1594.9 92.9 %all-reduce.14.cloned.1.call-done = f32[48,1152]{1,0:T(8,128)} async-done(((f32[48,1152]{1,0:T(8,128)}), f32[48,1152]{1,0:T(8,128)}) %all-reduce.14.cloned.1.call-update) | async-done | bytes 221200 | tf_op jit(solution)/shard_map/psum | solution.py:521
  1774.4 70.2 %all-reduce.18.cloned.1.call-done = (bf16[1152]{0:T(1024)(128)(2,1)}, bf16[8,1152]{1,0:T(8,128)(2,1)}, bf16[20,1152]{1,0:T(8,128)(2,1)}) async-done(((bf16[1152]{0:T(1024)(128)(2,1)}, bf16[8,1152]{1,0:T(8,128)(2,1)}, bf16[20,1152]{1,0:T(8,128)(2,1)}), (bf16[1152]{0:T(1024)(128)(2,1)}, bf16[8,1152]{1,0:T(8,128)(2,1)}, bf16[20,1152]{1,0:T(8,128)(2,1)})) %all-reduce.18.cloned.1.call-update) | async-done | bytes 66832 | tf_op jit(solution)/shard_map/psum | solution.py:554
  (746 shorter events, 789.0 us)
Async XLA Ops:
  41.3 143.8 %all-reduce.16.cloned.1.call-start = ((), (), s32[]{:S(2)}) async-start(), calls=%async_computation.53 | async-start | bytes 884736
  111.7 130.2 %all-gather.31.cloned.1.call-start = ((), (), s32[]{:S(2)}) async-start(), calls=%async_computation.17 | async-start | bytes 2985984 | tf_op jit(solution)/shard_map/all_gather | solution.py:264
  122.4 158.8 %reduce-scatter.26.cloned.1.call-start = ((), (), s32[]{:S(2)}) async-start(), calls=%async_computation.18 | async-start | bytes 1474560 | tf_op jit(solution)/shard_map/reduce_scatter | solution.py:195
  283.1 141.0 %all-gather.65.cloned.1.call-start = ((), (), s32[]{:S(2)}) async-start(), calls=%async_computation.47 | async-start | bytes 3981312 | tf_op jit(solution)/shard_map/all_gather | solution.py:266
  288.2 163.4 %reduce-scatter.28.cloned.1.call-start = ((), (), s32[]{:S(2)}) async-start(), calls=%async_computation.21 | async-start | bytes 1474560 | tf_op jit(solution)/shard_map/reduce_scatter | solution.py:195
  437.1 114.9 %all-gather.39.cloned.1.call-start = ((), (), s32[]{:S(2)}) async-start(), calls=%async_computation.24 | async-start | bytes 1474560 | tf_op jit(solution)/shard_map/all_gather | solution.py:201
  453.7 133.6 %reduce-scatter.32.cloned.1.call-start = ((), (), s32[]{:S(2)}) async-start(), calls=%async_computation.25 | async-start | bytes 1474560 | tf_op jit(solution)/shard_map/reduce_scatter | solution.py:195
  592.4 127.1 %all-gather.45.cloned.1.call-start = ((), (), s32[]{:S(2)}) async-start(), calls=%async_computation.28 | async-start | bytes 2985984 | tf_op jit(solution)/shard_map/all_gather | solution.py:269
  596.4 153.2 %reduce-scatter.34.cloned.1.call-start = ((), (), s32[]{:S(2)}) async-start(), calls=%async_computation.29 | async-start | bytes 1474560 | tf_op jit(solution)/shard_map/reduce_scatter | solution.py:195
  940.2 118.2 %reduce-scatter.46.cloned.1.call-start = ((), (), s32[]{:S(2)}) async-start(), calls=%async_computation.39 | async-start | bytes 2985984 | tf_op jit(solution)/shard_map/reduce_scatter | solution.py:397
  945.8 186.7 %reduce-scatter.42.cloned.1.call-start = ((), (), s32[]{:S(2)}) async-start(), calls=%async_computation.37 | async-start | bytes 2985984 | tf_op jit(solution)/shard_map/reduce_scatter | solution.py:397
  950.8 256.1 %reduce-scatter.54.cloned.1.call-start = ((), (), s32[]{:S(2)}) async-start(), calls=%async_computation.51 | async-start | bytes 2985984 | tf_op jit(solution)/shard_map/reduce_scatter | solution.py:397
  962.7 332.6 %reduce-scatter.56.cloned.1.call-start = ((), (), s32[]{:S(2)}) async-start(), calls=%async_computation.52 | async-start | bytes 4534272
  994.2 343.2 %reduce-scatter.44.cloned.1.call-start = ((), (), s32[]{:S(2)}) async-start(), calls=%async_computation.38 | async-start | bytes 1474560 | tf_op jit(solution)/shard_map/reduce_scatter | solution.py:195
  1008.1 373.7 %all-gather.63.cloned.1.call-start = ((), (), s32[]{:S(2)}) async-start(), calls=%async_computation.46 | async-start | bytes 1658880 | tf_op jit(solution)/shard_map/all_gather | solution.py:525
  1058.4 339.5 %all-gather.61.cloned.1.call-start = ((), (), s32[]{:S(2)}) async-start(), calls=%async_computation.45 | async-start | bytes 1658880 | tf_op jit(solution)/shard_map/all_gather | solution.py:525
  1132.6 281.4 %all-gather.59.cloned.1.call-start = ((), (), s32[]{:S(2)}) async-start(), calls=%async_computation.44 | async-start | bytes 1658880 | tf_op jit(solution)/shard_map/all_gather | solution.py:525
  1207.0 252.3 %reduce-scatter.52.cloned.1.call-start = ((), (), s32[]{:S(2)}) async-start(), calls=%async_computation.50 | async-start | bytes 2985984 | tf_op jit(solution)/shard_map/reduce_scatter | solution.py:397
  1218.7 262.5 %all-gather.67.cloned.1.call-start = ((), (), s32[]{:S(2)}) async-start(), calls=%async_computation.48 | async-start | bytes 2211840 | tf_op jit(solution)/shard_map/all_gather | solution.py:525
  1297.4 297.4 %reduce-scatter.50.cloned.1.call-start = ((), (), s32[]{:S(2)}) async-start(), calls=%async_computation.49 | async-start | bytes 2985984 | tf_op jit(solution)/shard_map/reduce_scatter | solution.py:397
  1309.1 378.8 %all-reduce.14.cloned.1.call-start = ((), (), s32[]{:S(2)}) async-start(), calls=%async_computation.41 | async-start | bytes 442368 | tf_op jit(solution)/shard_map/psum | solution.py:521
  1342.7 365.8 %all-gather.57.cloned.1.call-start = ((), (), s32[]{:S(2)}) async-start(), calls=%async_computation.43 | async-start | bytes 1658880 | tf_op jit(solution)/shard_map/all_gather | solution.py:525
  1459.3 269.1 %all-gather.55.cloned.1.call-start = ((), (), s32[]{:S(2)}) async-start(), calls=%async_computation.42 | async-start | bytes 1658880 | tf_op jit(solution)/shard_map/all_gather | solution.py:525
  1594.8 249.7 %all-reduce.18.cloned.1.call-start = ((), (), s32[]{:S(2)}) async-start(), calls=%async_computation.54 | async-start | bytes 155648 | tf_op jit(solution)/shard_map/psum | solution.py:554
  (166 other events, 6121.6 us)
Sparse Core Ops, SparseCore 0:
  41.4 67.4 all-reduce.11
  112.9 72.1 all-reduce.15
  187.8 54.0 all-gather.30
  256.9 24.1 reduce-scatter.25
  283.7 54.9 all-gather.34
  359.5 64.5 all-gather.64
  427.3 24.3 reduce-scatter.27
  478.8 54.9 all-gather.36
  561.7 25.5 reduce-scatter.31
  589.5 54.9 all-gather.42
  664.5 54.9 all-gather.44
  725.3 24.1 reduce-scatter.33
  787.5 25.5 reduce-scatter.35
  847.3 25.5 reduce-scatter.37
  912.6 25.5 reduce-scatter.39
  986.5 71.7 reduce-scatter.45
  1061.8 70.6 reduce-scatter.41
  1136.6 70.2 reduce-scatter.53
  1211.1 84.1 reduce-scatter.55
  1298.5 25.2 reduce-scatter.43
  1388.0 71.2 reduce-scatter.51
  1485.4 72.8 reduce-scatter.49
  1564.3 123.5 all-reduce.13
  1774.3 70.1 all-reduce.17
  (15 shorter events, 273.7 us)

commit v2 on v1

--- a/solution.py
+++ b/solution.py
@@ -3,6 +3,8 @@
 import jax
 import jax.numpy as jnp
 from jax import lax
+from jax.experimental import pallas as pl
+from jax.experimental.pallas import tpu as pltpu
 from jax.sharding import PartitionSpec as P
 
 HEAD_DIM = 72
@@ -191,14 +193,250 @@
     return (new_weight, new_weight.astype(jnp.bfloat16), clipped)
 
 
-def token_sum(pieces):
-    return lax.psum_scatter(
-        pieces.astype(jnp.bfloat16), "mp", scatter_dimension=0, tiled=True
-    ).astype(jnp.float32)
-
-
-def token_gather(rows):
-    return lax.all_gather(rows, "mp", axis=0, tiled=True)
+MESH_ID = pl.DeviceIdType.MESH
+ROW_STEP = 16
+
+
+def remote(source, target, send_sem, recv_sem, device):
+    return pltpu.make_async_remote_copy(
+        src_ref=source,
+        dst_ref=target,
+        send_sem=send_sem,
+        recv_sem=recv_sem,
+        device_id=device,
+        device_id_type=MESH_ID,
+    )
+
+
+def greet(devices):
+    barrier = pltpu.get_barrier_semaphore()
+    for device in devices:
+        pl.semaphore_signal(barrier, inc=1, device_id=device, device_id_type=MESH_ID)
+    pl.semaphore_wait(barrier, len(devices))
+
+
+def exchange(axis, arrays, shared, number):
+    size = lax.axis_size(axis)
+    count = len(arrays)
+
+    def kernel(*refs):
+        sources, results = refs[0:count], refs[count : 2 * count]
+        send_sem, recv_sem = refs[2 * count :]
+        me = lax.axis_index(axis)
+        peers = [lax.rem(me + step, size) for step in range(1, size)]
+        greet([{axis: peer} for peer in peers])
+        copies = []
+        for step, peer in enumerate(peers):
+            for at in range(count):
+                source = sources[at] if shared[at] else sources[at].at[peer]
+                copy = remote(
+                    source,
+                    results[at].at[me],
+                    send_sem.at[at, step],
+                    recv_sem.at[at, step],
+                    {axis: peer},
+                )
+                copy.start()
+                copies.append(copy)
+        for at in range(count):
+            own = sources[at][...] if shared[at] else sources[at][me]
+            results[at][me] = own
+        for copy in copies:
+            copy.wait()
+
+    shapes = [
+        jax.ShapeDtypeStruct((size,) + (array.shape if keep else array.shape[1:]), array.dtype)
+        for array, keep in zip(arrays, shared)
+    ]
+    vmem = pl.BlockSpec(memory_space=pltpu.VMEM)
+    return pl.pallas_call(
+        kernel,
+        out_shape=shapes,
+        in_specs=[vmem] * count,
+        out_specs=[vmem] * count,
+        scratch_shapes=[
+            pltpu.SemaphoreType.DMA((count, size - 1)),
+            pltpu.SemaphoreType.DMA((count, size - 1)),
+        ],
+        compiler_params=pltpu.CompilerParams(collective_id=number, has_side_effects=True),
+        name=f"exchange_{axis}_{number}",
+    )(*arrays)
+
+
+def across(pieces, own, step_rows, row_types, sums, gather, number):
+    size = lax.axis_size("mp")
+    chips = size // 2
+    adds = pieces is not None
+    rows = pieces.shape[0] // size if adds else own[0].shape[0]
+    width = own[0].shape[1] if own else pieces.shape[1]
+    bfloat = jnp.bfloat16
+    n_own, n_rows = len(own), len(row_types)
+
+    def kernel(*refs):
+        refs = list(refs)
+        if adds:
+            part = refs.pop(0)
+        owns, refs = refs[0:n_own], refs[n_own:]
+        row_refs, refs = refs[0:n_rows], refs[n_rows:]
+        sum_refs, refs = refs[0:sums], refs[sums:]
+        if gather:
+            full = refs.pop(0)
+        if adds:
+            near, away, far, near_send, near_recv, far_send, far_recv = refs[0:7]
+            refs = refs[7:]
+        me = lax.axis_index("mp")
+        core = lax.rem(me, 2)
+        chip = me // 2
+        partner = me + 1 - 2 * core
+
+        def device(number_at):
+            return {"mp": number_at}
+
+        def at_step(step):
+            return lax.rem(chip + step, chips)
+
+        def block(number_at):
+            return pl.ds(pl.multiple_of(number_at * rows, rows), rows)
+
+        greet([device(partner)] + [device(at_step(k) * 2 + core) for k in range(1, chips)])
+        pending = []
+        if adds:
+            near_copies = {}
+            for k in list(range(1, chips)) + [0]:
+                copy = remote(
+                    part.at[block(at_step(k) * 2 + 1 - core)],
+                    near.at[k],
+                    near_send.at[k],
+                    near_recv.at[k],
+                    device(partner),
+                )
+                copy.start()
+                near_copies[k] = copy
+                pending.append(copy)
+            far_copies = []
+            for k in range(1, chips):
+                near_copies[k].wait_recv()
+                start = (at_step(k) * 2 + core) * rows
+
+                @pl.loop(0, rows // ROW_STEP)
+                def _(i):
+                    here = pl.ds(pl.multiple_of(i * ROW_STEP, ROW_STEP), ROW_STEP)
+                    there = pl.ds(pl.multiple_of(start + i * ROW_STEP, ROW_STEP), ROW_STEP)
+                    away[k - 1, here] = (
+                        part[there].astype(jnp.float32) + near[k, here].astype(jnp.float32)
+                    ).astype(bfloat)
+
+                copy = remote(
+                    away.at[k - 1],
+                    far.at[k - 1],
+                    far_send.at[k - 1],
+                    far_recv.at[k - 1],
+                    device(at_step(k) * 2 + core),
+                )
+                copy.start()
+                far_copies.append(copy)
+                pending.append(copy)
+            near_copies[0].wait_recv()
+            for copy in far_copies:
+                copy.wait_recv()
+        for ref in sum_refs:
+            ref[...] = jnp.zeros_like(ref)
+        mine = me * rows
+
+        @pl.loop(0, rows // ROW_STEP)
+        def _(i):
+            here = pl.ds(pl.multiple_of(i * ROW_STEP, ROW_STEP), ROW_STEP)
+            there = pl.ds(pl.multiple_of(mine + i * ROW_STEP, ROW_STEP), ROW_STEP)
+            values = [ref[here] if ref.shape[0] == rows else ref[...] for ref in owns]
+            if adds:
+                total = part[there].astype(jnp.float32) + near[0, here].astype(jnp.float32)
+                for k in range(1, chips):
+                    total = total + far[k - 1, here].astype(jnp.float32)
+                row_values, terms, sent = step_rows(total, *values)
+            else:
+                row_values, terms, sent = [], [], values[0]
+            for ref, value in zip(row_refs, row_values):
+                ref[here] = value.astype(ref.dtype)
+            for ref, value in zip(sum_refs, terms):
+                ref[...] += jnp.sum(value.reshape(ROW_STEP // 8, 8, width), axis=0)
+            if gather:
+                full[there] = sent.astype(bfloat)
+
+        if gather:
+            out_send, out_recv, back_send, back_recv = refs
+            outward = []
+            for k in list(range(1, chips)) + [0]:
+                copy = remote(
+                    full.at[block(me)],
+                    full.at[block(me)],
+                    out_send.at[k],
+                    out_recv.at[k],
+                    device(at_step(k) * 2 + core) if k else device(partner),
+                )
+                copy.start()
+                outward.append(copy)
+                pending.append(copy)
+            backward = []
+            for k in range(1, chips):
+                outward[k - 1].wait_recv()
+                came = at_step(chips - k) * 2 + core
+                copy = remote(
+                    full.at[block(came)],
+                    full.at[block(came)],
+                    back_send.at[k - 1],
+                    back_recv.at[k - 1],
+                    device(partner),
+                )
+                copy.start()
+                backward.append(copy)
+                pending.append(copy)
+            outward[-1].wait_recv()
+            for copy in backward:
+                copy.wait_recv()
+        for copy in pending:
+            copy.wait_send()
+
+    dma = pltpu.SemaphoreType.DMA
+    shapes = [jax.ShapeDtypeStruct((rows, width), kind) for kind in row_types]
+    shapes += [jax.ShapeDtypeStruct((8, width), jnp.float32)] * sums
+    scratch = []
+    if gather:
+        shapes.append(jax.ShapeDtypeStruct((rows * size, width), bfloat))
+    if adds:
+        scratch += [
+            pltpu.VMEM((chips, rows, width), bfloat),
+            pltpu.VMEM((chips - 1, rows, width), bfloat),
+            pltpu.VMEM((chips - 1, rows, width), bfloat),
+            dma((chips,)),
+            dma((chips,)),
+            dma((chips - 1,)),
+            dma((chips - 1,)),
+        ]
+    if gather:
+        scratch += [dma((chips,)), dma((chips,)), dma((chips - 1,)), dma((chips - 1,))]
+    vmem = pl.BlockSpec(memory_space=pltpu.VMEM)
+    inputs = ([pieces] if adds else []) + list(own)
+    return pl.pallas_call(
+        kernel,
+        out_shape=shapes,
+        in_specs=[vmem] * len(inputs),
+        out_specs=[vmem] * len(shapes),
+        scratch_shapes=scratch,
+        compiler_params=pltpu.CompilerParams(collective_id=number, has_side_effects=True),
+        name=f"across_{number}",
+    )(*inputs)
+
+
+def normalize(values):
+    center = values - jnp.mean(values, axis=-1, keepdims=True)
+    spread = lax.rsqrt(jnp.mean(center * center, axis=-1, keepdims=True) + norm_eps)
+    return center * spread, spread
+
+
+def normalize_grad(normal, spread, grad_rows):
+    mean_grad = jnp.mean(grad_rows, axis=-1, keepdims=True)
+    mean_both = jnp.mean(grad_rows * normal, axis=-1, keepdims=True)
+    return spread * (grad_rows - mean_grad - normal * mean_both)
 
 
 def pad_samples(rows):
@@ -284,18 +522,35 @@
     def own_cols(rows):
         return lax.dynamic_slice_in_dim(rows, row_start, row_count_own, 1)
 
-    all_times = lax.all_gather(timesteps, "dp", axis=0, tiled=True)
+    numbers = jnp.zeros((8, 128), jnp.int32)
+    numbers = numbers.at[0, 0:SLOTS].set(timesteps).at[0, SLOTS].set(counts[0])
+    numbers_all = exchange("dp", [numbers], [True], 1)[0]
+    all_times = numbers_all[:, 0, 0:SLOTS].reshape(-1)
+    count_total = jnp.sum(numbers_all[:, 0, SLOTS]).astype(jnp.float32)
     alpha_now, rest_now, beta_now, posterior, kappa = plan(timesteps)
     features = time_features(all_times).astype(bfloat)
     first_pre = product(features, freq_w)
     first_act = jax.nn.silu(first_pre).astype(bfloat)
-    time_emb_all = lax.psum(product(own_cols(first_act), temb_rows), "dp")
-    temb_act = jax.nn.silu(time_emb_all).astype(bfloat)
-    mod_part = contract("sd,kde->ske", own_cols(temb_act), mod_rows)
+    temb_part = product(own_cols(first_act), temb_rows)
+    sample_count = temb_part.shape[0]
+    temb_cols_all, temb_rows_all = exchange(
+        "dp",
+        [
+            temb_part.reshape(sample_count, dp_size, row_count_own).transpose(1, 0, 2),
+            temb_part.reshape(dp_size, SLOTS, D),
+        ],
+        [False, False],
+        2,
+    )
+    time_cols = jnp.sum(temb_cols_all, axis=0)
+    time_emb = jnp.sum(temb_rows_all, axis=0)
+    temb_act = jax.nn.silu(time_cols).astype(bfloat)
+    mod_part = contract("sd,kde->ske", temb_act, mod_rows)
     modulation = (
-        lax.psum_scatter(mod_part, "dp", scatter_dimension=0, tiled=True) + tables[None, 0:6]
-    )
-    time_emb = lax.dynamic_slice_in_dim(time_emb_all, dp_index * SLOTS, SLOTS, 0)
+        jnp.sum(exchange("dp", [mod_part.reshape(dp_size, SLOTS * 6, D)], [False], 3)[0], axis=0)
+        .reshape(SLOTS, 6, D)
+        + tables[None, 0:6]
+    )
     mods_own = lax.dynamic_index_in_dim(modulation, sample, 0, keepdims=False)
     shift_a, scale_a, gate_a, shift_b, scale_b, gate_b = [
         mods_own[number : number + 1] for number in range(6)
@@ -316,8 +571,10 @@
     cap_rows = captions.reshape(SLOTS * CAP_LEN, CAP_DIM)
     cap_mid = product(cap_rows, full_cap)
     cap_act = gelu_tanh(cap_mid).astype(bfloat)
-    context_own = token_sum(pad_samples(contract("re,de->rd", cap_act, full_c2))).astype(bfloat)
-    context_low = cut_samples(token_gather(context_own))
+    context_part = pad_samples(contract("re,de->rd", cap_act, full_c2).astype(bfloat))
+    context_low = cut_samples(
+        across(context_part, [], lambda total: ([], [], total), [], 0, True, 4)[0]
+    )
 
     normed_a = (
         modulate(start_hidden, modulation[:, 0][:, None], modulation[:, 1][:, None])
@@ -328,22 +585,45 @@
     qkv_s = [spatial_heads(qkv[:, k * lw : (k + 1) * lw], head_count) for k in range(3)]
     mixed_s, logsum_s = attend_forward(*qkv_s)
     mixed_s_low = mixed_s.astype(bfloat).reshape(TOK_DEV, lw)
-    branch_s = token_sum(contract("te,de->td", mixed_s_low, full_s[:, 3 * lw :]))
-    hidden_s = start_own + gate_a * branch_s
     frame_start = (token_start % per_sample) // PATCHES
     frames_own = own_tokens // PATCHES
     temporal_own = lax.dynamic_slice_in_dim(temporal_pos, frame_start, frames_own, 0)
-    timed_own = (
-        hidden_s.reshape(frames_own, PATCHES, D) + temporal_own[:, None, :]
-    ).astype(bfloat)
-    timed_low = token_gather(timed_own.reshape(own_tokens, D))
+    temporal_rows = jnp.broadcast_to(
+        temporal_own[:, None, :], (frames_own, PATCHES, D)
+    ).reshape(own_tokens, D)
+
+    def spatial_step(total, start_rows, gate, position):
+        hidden = start_rows + gate * total
+        return [total, hidden], [], hidden + position
+
+    f32 = jnp.float32
+    branch_s, hidden_s, timed_low = across(
+        contract("te,de->td", mixed_s_low, full_s[:, 3 * lw :]).astype(bfloat),
+        [start_own, gate_a, temporal_rows],
+        spatial_step,
+        [f32, f32],
+        0,
+        True,
+        5,
+    )
     qkv = product(timed_low, full_t[:, 0 : 3 * lw]).astype(bfloat)
     qkv_t = [temporal_heads(qkv[:, k * lw : (k + 1) * lw], head_count) for k in range(3)]
     mixed_t, logsum_t = attend_forward(*qkv_t)
     mixed_t_low = from_frames(mixed_t.astype(bfloat)[None], head_count)[0]
-    branch_t = token_sum(contract("te,de->td", mixed_t_low, full_t[:, 3 * lw :]))
-    hidden_t = hidden_s + gate_a * branch_t
-    hidden_low = token_gather(hidden_t.astype(bfloat))
+
+    def temporal_step(total, hidden_rows, gate):
+        hidden = hidden_rows + gate * total
+        return [total, hidden], [], hidden
+
+    branch_t, hidden_t, hidden_low = across(
+        contract("te,de->td", mixed_t_low, full_t[:, 3 * lw :]).astype(bfloat),
+        [hidden_s, gate_a],
+        temporal_step,
+        [f32, f32],
+        0,
+        True,
+        6,
+    )
     query_c = (
         product(hidden_low, full_c[:, 0:lw])
         .astype(bfloat)
@@ -354,15 +634,38 @@
     value_c = key_value[:, lw:].reshape(SLOTS, CAP_LEN, head_count, HEAD_DIM)
     mixed_c, logsum_c = attend_forward(query_c, key_c, value_c)
     mixed_c_low = mixed_c.astype(bfloat).reshape(TOK_DEV, lw)
-    hidden_c = hidden_t + token_sum(contract("te,de->td", mixed_c_low, full_c[:, 3 * lw :]))
-    normed_b = token_gather(modulate(hidden_c, shift_b, scale_b).astype(bfloat))
+
+    def cross_step(total, hidden_rows, shift, scale):
+        hidden = hidden_rows + total
+        return [hidden], [], normalize(hidden)[0] * (1.0 + scale) + shift
+
+    hidden_c, normed_b = across(
+        contract("te,de->td", mixed_c_low, full_c[:, 3 * lw :]).astype(bfloat),
+        [hidden_t, shift_b, scale_b],
+        cross_step,
+        [f32],
+        0,
+        True,
+        7,
+    )
     inner_pre = product(normed_b, full_i)
     inner_act = gelu_tanh(inner_pre).astype(bfloat)
-    branch_m = token_sum(contract("te,de->td", inner_act, full_o))
-    hidden_m = hidden_c + gate_b * branch_m
     shift_f = tables[6:7] + temb_own
     scale_f = tables[7:8] + temb_own
-    normed_f = modulate(hidden_m, shift_f, scale_f).astype(bfloat)
+
+    def forward_step(total, hidden_rows, gate, shift, scale):
+        hidden = hidden_rows + gate * total
+        return [total, hidden, normalize(hidden)[0] * (1.0 + scale) + shift], [], None
+
+    branch_m, hidden_m, normed_f = across(
+        contract("te,de->td", inner_act, full_o).astype(bfloat),
+        [hidden_c, gate_b, shift_f, scale_f],
+        forward_step,
+        [f32, f32, bfloat],
+        0,
+        False,
+        8,
+    )
     output = contract("td,od->to", normed_f, final_w).reshape(own_tokens, 4, 8)
     target = own_rows(gaussian_noise.reshape(TOK_DEV, 4, 4))
     error_rows = output[:, :, 0:4] - target
@@ -387,7 +690,9 @@
     grad_normed = contract("to,od->td", grad_output, final_w)
     grad_hidden, grad_shift_f, grad_scale_f = modulate_grad(hidden_m, shift_f, scale_f, grad_normed)
     grad_gate_b = jnp.sum(grad_hidden * branch_m, axis=0, keepdims=True)
-    grad_branch = token_gather((gate_b * grad_hidden).astype(bfloat))
+    grad_branch = across(
+        None, [(gate_b * grad_hidden).astype(bfloat)], None, [], 0, True, 9
+    )[0]
     grad_inner = act_grad(gelu_tanh, inner_pre, product(grad_branch, full_o)).astype(bfloat)
     part = contract("te,de->td", grad_inner, full_i)
     grad_pack_o = contract("td,te->de", grad_branch, inner_act)
@@ -400,10 +705,24 @@
 
     sum_o = row_sum(grad_pack_o)
     sum_i = row_sum(grad_pack_i)
-    grad_normed = token_sum(part)
-    grad_more, grad_shift_b, grad_scale_b = modulate_grad(hidden_c, shift_b, scale_b, grad_normed)
-    grad_hidden = grad_hidden + grad_more
-    grad_branch = token_gather(grad_hidden.astype(bfloat))
+
+    def forward_grad_step(total, hidden_rows, scale, grad_rows):
+        normal, spread = normalize(hidden_rows)
+        grad = grad_rows + normalize_grad(normal, spread, total * (1.0 + scale))
+        return [grad], [total, total * normal], grad
+
+    def one_row(rows):
+        return jnp.sum(rows, axis=0, keepdims=True)
+
+    grad_hidden, grad_shift_b, grad_scale_b, grad_branch = across(
+        part.astype(bfloat),
+        [hidden_c, scale_b, grad_hidden],
+        forward_grad_step,
+        [f32],
+        2,
+        True,
+        10,
+    )
     grad_mixed = (
         product(grad_branch, full_c[:, 3 * lw :])
         .astype(bfloat)
@@ -432,9 +751,14 @@
             axis=1,
         )
     )
-    grad_hidden = grad_hidden + token_sum(part)
-    grad_gate_a = jnp.sum(grad_hidden * branch_t, axis=0, keepdims=True)
-    grad_branch = token_gather((gate_a * grad_hidden).astype(bfloat))
+
+    def gated_step(total, grad_rows, branch_rows, gate):
+        grad = grad_rows + total
+        return [grad], [grad * branch_rows], gate * grad
+
+    grad_hidden, grad_gate_t, grad_branch = across(
+        part.astype(bfloat), [grad_hidden, branch_t, gate_a], gated_step, [f32], 1, True, 11
+    )
     grad_mixed = temporal_heads(
         product(grad_branch, full_t[:, 3 * lw :]).astype(bfloat), head_count
     )
@@ -451,9 +775,9 @@
             axis=1,
         )
     )
-    grad_hidden = grad_hidden + token_sum(part)
-    grad_gate_a = grad_gate_a + jnp.sum(grad_hidden * branch_s, axis=0, keepdims=True)
-    grad_branch = token_gather((gate_a * grad_hidden).astype(bfloat))
+    grad_hidden, grad_gate_s, grad_branch = across(
+        part.astype(bfloat), [grad_hidden, branch_s, gate_a], gated_step, [f32], 1, True, 12
+    )
     grad_mixed = spatial_heads(
         product(grad_branch, full_s[:, 3 * lw :]).astype(bfloat), head_count
     )
@@ -472,7 +796,15 @@
         )
     )
     grad_context = cut_samples(
-        token_gather(token_sum(pad_samples(part_context)).astype(bfloat))
+        across(
+            pad_samples(part_context.astype(bfloat)),
+            [],
+            lambda total: ([], [], total),
+            [],
+            0,
+            True,
+            13,
+        )[0]
     )
     grad_cap2 = contract("rd,re->de", grad_context, cap_act)
     grad_cap_mid = act_grad(
@@ -488,37 +820,70 @@
             axis=1,
         ).reshape(dp_size * (cap_rows_own + row_count_own), lw)
     )
-    grad_normed = token_sum(part)
-    grad_more, grad_shift_a, grad_scale_a = modulate_grad(start_own, shift_a, scale_a, grad_normed)
-    grad_hidden = grad_hidden + grad_more
-    grad_patch = contract("ti,td->id", own_rows(patches), grad_hidden.astype(bfloat))
+
+    def start_grad_step(total, hidden_rows, scale, grad_rows):
+        normal, spread = normalize(hidden_rows)
+        grad = grad_rows + normalize_grad(normal, spread, total * (1.0 + scale))
+        return [grad], [total, total * normal], None
+
+    grad_start, grad_shift_a, grad_scale_a = across(
+        part.astype(bfloat),
+        [start_own, scale_a, grad_hidden],
+        start_grad_step,
+        [bfloat],
+        2,
+        False,
+        14,
+    )
+    grad_patch = contract("ti,td->id", own_rows(patches), grad_start)
     grad_mods = jnp.concatenate(
         [
-            grad_shift_a, grad_scale_a, grad_gate_a, grad_shift_b, grad_scale_b, grad_gate_b,
+            one_row(grad_shift_a), one_row(grad_scale_a), one_row(grad_gate_t + grad_gate_s),
+            one_row(grad_shift_b), one_row(grad_scale_b), grad_gate_b,
             grad_shift_f, grad_scale_f,
         ],
         axis=0,
     )
     placed = jnp.where(
         (jnp.arange(SLOTS) == sample)[:, None, None], grad_mods[None], 0.0
-    )
-    grad_mods = lax.psum(placed, "mp")
-    mods_all = lax.all_gather(grad_mods.astype(bfloat), "dp", axis=0, tiled=True)
+    ).reshape(SLOTS * 8, D)
+    small_rows_part = jnp.concatenate([grad_patch, grad_final], axis=0)
+    small_count = small_rows_part.shape[0] // mp_size
+    loss_block = jnp.broadcast_to(loss_local, (8, 128))
+    placed_all, small_all, loss_all = exchange(
+        "mp",
+        [placed, small_rows_part.reshape(mp_size, small_count, D), loss_block],
+        [True, False, True],
+        15,
+    )
+    grad_mods = jnp.sum(placed_all, axis=0).reshape(SLOTS, 8, D)
+    small_own = jnp.sum(small_all, axis=0).astype(bfloat)
+    loss_part = jnp.sum(loss_all[:, 0, 0])
+    mods_all, small_all = exchange(
+        "dp", [grad_mods.astype(bfloat).reshape(SLOTS * 8, D), small_own], [True, True], 16
+    )
+    mods_all = mods_all.reshape(dp_size * SLOTS, 8, D)
+    small_own = jnp.sum(small_all.astype(f32), axis=0)
     grad_mods_low = mods_all[:, 0:6]
-    grad_tables = jnp.sum(mods_all.astype(jnp.float32), axis=0)
+    grad_tables = jnp.sum(mods_all.astype(f32), axis=0)
     grad_temb_act = contract("ske,kde->sd", grad_mods_low, mod_rows)
-    grad_temb = act_grad(jax.nn.silu, own_cols(time_emb_all), grad_temb_act) + own_cols(
-        (mods_all[:, 6].astype(jnp.float32) + mods_all[:, 7].astype(jnp.float32))
-    )
-    grad_temb_low = lax.all_gather(grad_temb.astype(bfloat), "dp", axis=1, tiled=True)
+    grad_temb = act_grad(jax.nn.silu, time_cols, grad_temb_act) + own_cols(
+        (mods_all[:, 6].astype(f32) + mods_all[:, 7].astype(f32))
+    )
+
+    def dp_columns(rows, number):
+        blocks = exchange("dp", [rows], [True], number)[0]
+        return blocks.transpose(1, 0, 2).reshape(rows.shape[0], D)
+
+    grad_temb_low = dp_columns(grad_temb.astype(bfloat), 17)
     grad_first_own = act_grad(
         jax.nn.silu, own_cols(first_pre), contract("sd,id->si", grad_temb_low, temb_rows)
     ).astype(bfloat)
-    grad_first = lax.all_gather(grad_first_own, "dp", axis=1, tiled=True)
-    grad_time = contract("sd,ske->kde", own_cols(temb_act), grad_mods_low)
+    grad_first = dp_columns(grad_first_own, 18)
+    grad_time = contract("sd,ske->kde", temb_act, grad_mods_low)
     grad_temb_part = contract("si,sd->id", own_cols(first_act), grad_temb_low)
     grad_freq = contract("sf,sd->fd", features, grad_first)
-    small_part = lax.psum(jnp.concatenate([grad_patch, grad_final], axis=0), ("dp", "mp"))
+    small_part = exchange("mp", [small_own], [True], 19)[0].reshape(mp_size * small_count, D)
     sum_small = jnp.concatenate([small_part[0:16], grad_freq, grad_tables, small_part[16:]], axis=0)
 
     def all_columns(rows):
@@ -538,7 +903,6 @@
         [whole_s[3:4], whole_t[3:4], whole_c[3:4], whole_o, whole_x[:, cap_rows_own:]], axis=0
     )
     sum_cap = whole_x[0, 0:cap_rows_own]
-    count_local = counts[0].astype(jnp.float32)
     square_in = sum_in * sum_in
     square_out = sum_out * sum_out
     square_cap = sum_cap * sum_cap
@@ -548,13 +912,17 @@
     row_cap_total = jnp.sum(square_cap, axis=1)
     row_small_total = jnp.sum(square_small, axis=1)
     col_small_total = jnp.sum(square_small, axis=0)
-    col_in_total, col_out_total, col_cap_total, loss_total, count_total = (
-        lax.psum(jnp.sum(square_in, axis=1).astype(jnp.bfloat16), "dp").astype(jnp.float32),
-        lax.psum(jnp.sum(square_out, axis=1).astype(jnp.bfloat16), "dp").astype(jnp.float32),
-        lax.psum(jnp.sum(square_cap, axis=0).astype(jnp.bfloat16), "dp").astype(jnp.float32),
-        lax.psum(loss_local, ("dp", "mp")),
-        lax.psum(count_local, "dp"),
-    )
+    col_part = jnp.concatenate(
+        [
+            jnp.sum(square_in, axis=1),
+            jnp.sum(square_out, axis=1),
+            jnp.sum(square_cap, axis=0, keepdims=True),
+        ],
+        axis=0,
+    )
+    col_all = exchange("dp", [col_part.astype(bfloat)], [True], 20)[0]
+    col_total = jnp.sum(col_all.astype(f32), axis=0)
+    col_in_total, col_out_total, col_cap_total = col_total[0:20], col_total[20:28], col_total[28]
     inverse = 1.0 / count_total
     inverse_sq = inverse * inverse
     rows_in_new = new_stat(rows_in, row_in_total, D, inverse_sq)
@@ -569,17 +937,18 @@
     grad_out = sum_out * inverse
     grad_cap_all = (sum_cap * inverse)[None]
     grad_small_all = (sum_small * inverse)[None]
-    ratios = lax.psum(
-        jnp.concatenate(
-            [
-                ratio_terms(w_in, grad_in, rows_in_new, cols_in_new),
-                ratio_terms(w_out, grad_out, rows_out_new, cols_out_new),
-                ratio_terms(w_cap[None], grad_cap_all, rows_cap_new[None], cols_cap_new[None]),
-            ],
-            axis=1,
-        ),
-        "dp",
-    )
+    ratio_part = jnp.concatenate(
+        [
+            ratio_terms(w_in, grad_in, rows_in_new, cols_in_new),
+            ratio_terms(w_out, grad_out, rows_out_new, cols_out_new),
+            ratio_terms(w_cap[None], grad_cap_all, rows_cap_new[None], cols_cap_new[None]),
+        ],
+        axis=1,
+    )
+    ratio_block = jnp.zeros((8, 128), f32).at[0:3, 0:29].set(ratio_part).at[3, 0].set(loss_part)
+    ratio_block = jnp.sum(exchange("dp", [ratio_block], [True], 21)[0], axis=0)
+    ratios = ratio_block[0:3, 0:29]
+    loss_total = ratio_block[3, 0]
     totals = jnp.concatenate(
         [
             ratios,

time: 1950 us -> 1330 us (0.68)
  waiting for transfers between devices: 1180 us -> 374 us
  Pallas kernels: 0 us -> 356 us
  blocking collectives: 212 us -> 0 us
  local copies, waits for them, and re-layouts: 240 us -> 285 us
    pallas_call x0 -> x21, Pallas kernels: none -> 356 us  [the longest x11 219 us: across(): pl.pallas_call(kernel, out_shape=shapes, in_specs=[vmem] * len(inputs), o...]
    psum x3 -> x0, waiting for transfers between devices: 219 us -> none  [the longest x1 92.9 us: shards(): lax.psum(jnp.concatenate([grad_patch, grad_final], axis=0), ('dp', 'mp'))]
    reduce_scatter x10 -> x0, waiting for transfers between devices: 165 us -> none  [token_sum(): lax.psum_scatter(pieces.astype(jnp.bfloat16), 'mp', scatter_dimension=0,...]
    all_gather x5 -> x0, blocking collectives: 108 us -> none  [the longest x1 32.4 us: shards(): lax.all_gather(grad_mods.astype(bfloat), 'dp', axis=0, tiled=True)]
    all_gather x7 -> x0, waiting for transfers between devices: 100 us -> none  [token_gather(): return lax.all_gather(rows, 'mp', axis=0, tiled=True)]
    psum x4 -> x0, blocking collectives: 90.1 us -> none  [the longest x1 37.6 us: shards(): lax.psum(loss_local, ('dp', 'mp'))]
    all_gather x1, waiting for transfers between devices: 52.9 us -> 0.01 us  [shards(): full_s = lax.all_gather(pack_s, 'dp', axis=0, tiled=True)]
    all_gather x1, waiting for transfers between devices: 50.1 us -> 0.02 us  [shards(): full_t = lax.all_gather(pack_t, 'dp', axis=0, tiled=True)]
  transfers between devices with their start and end apart: 39 -> 18, of which waited for: 33 -> 11; matrix products, arithmetic and copies ran while one was open for 15% -> 27% of each run, Pallas kernels for 0% -> 17%
where the time goes in v2:
time: 1330 us; the launch traced here: 1310 us
  waiting for transfers between devices  374 us (28%)
  Pallas kernels  356 us (27%)
  local copies, waits for them, and re-layouts  285 us (21%)
  other arithmetic  141 us (11%)
  matrix products  131 us (10%)
  between operations  24.2 us (2%)
    pallas_call x11, Pallas kernels, across(): pl.pallas_call(kernel, out_shape=shapes, in_specs=[vmem] * len(inputs), o...  219 us
    reduce_scatter x5, waiting for transfers between devices, row_sum(): lax.psum_scatter(pieces.astype(bfloat), 'dp', scatter_dimension=0, tiled=...  176 us
    pallas_call x10, Pallas kernels, exchange(): pl.pallas_call(kernel, out_shape=shapes, in_specs=[vmem] * count, out_spe...  137 us
    dot_general x49, matrix products, contract(): return jnp.einsum(form, left, right, preferred_element_type=jnp.float32)  92.6 us
    unnamed x19, waiting for transfers between devices  82.7 us
    unnamed x295, local copies, waits for them, and re-layouts  74.3 us
    convert_element_type x9, local copies, waits for them, and re-layouts, shards(): all_columns(rows).astype(jnp.float32)  47.7 us
    all_gather x1, waiting for transfers between devices, shards(): full_x = lax.all_gather(pack_x, 'dp', axis=0, tiled=False)  45.1 us
  transfers between devices with their start and end apart: 18, of which 11 were waited for; matrix products, arithmetic and copies ran while one was open for 27% of the time, Pallas kernels for 17%

profile of v2, /device:TPU:0, one launch (start us, length us, event | category | flops | bytes accessed | tf_op | source)
XLA Modules:
  0.0 1313.8 jit_solution(12935294065122807909)
XLA Ops:
  75.9 11.8 exchange_dp_2.1
  92.1 23.5 %exchange_dp_3.1 = f32[8,12,1152]{2,1,0:T(8,128)} custom-call(f32[8,12,1152]{2,1,0:T(8,128)} %reshape.883.refs_0_), custom_call_target="tpu_custom_call" | custom-call | tf_op jit(solution)/shard_map/exchange_dp_3/pallas_call | solution.py:252
  149.6 23.3 %across_5.1 = (f32[128,1152]{1,0:T(8,128)}, f32[128,1152]{1,0:T(8,128)}, bf16[512,1152]{1,0:T(8,128)(2,1)}) custom-call(bf16[512,1152]{1,0:T(8,128)(2,1)} %convolution_convert_fusion.13.refs_0_, f32[128,1152]{1,0:T(8,128)} %constant_dynamic-slice_fusion.5.refs_1_, f32[1,1152]{1,0:T(1,128)} %get-tuple-element.292.refs_2_.refs_3_, f32[128,1152]{1,0:T(8,128)} %bitcast.377), custom_call_target="tpu_custom_call" | custom-call | tf_op jit(solution)/shard_map/across_5/pallas_call | solution.py:419
  199.4 23.7 %across_6.1 = (f32[128,1152]{1,0:T(8,128)}, f32[128,1152]{1,0:T(8,128)}, bf16[512,1152]{1,0:T(8,128)(2,1)}) custom-call(bf16[512,1152]{1,0:T(8,128)(2,1)} %convolution_convert_fusion.12.refs_0_, f32[128,1152]{1,0:T(8,128)} %get-tuple-element.103.refs_1_, f32[1,1152]{1,0:T(1,128)} %get-tuple-element.292.refs_2_.refs_3_), custom_call_target="tpu_custom_call" | custom-call | tf_op jit(solution)/shard_map/across_6/pallas_call | solution.py:419
  230.7 45.1 %all-gather.42.cloned.1.call-done = bf16[8,656,288]{1,2,0:T(8,128)(2,1)} async-done(((bf16[1,656,288]{1,2,0:T(8,128)(2,1)}), bf16[8,656,288]{1,2,0:T(8,128)(2,1)}) %all-gather.42.cloned.1.call-update) | async-done | bytes 3022864 | tf_op jit(solution)/shard_map/all_gather | solution.py:504
  285.4 15.8 %across_4.1 = bf16[256,1152]{1,0:T(8,128)(2,1)} custom-call(bf16[256,1152]{1,0:T(8,128)(2,1)} %bitcast.376), custom_call_target="tpu_custom_call" | custom-call | tf_op jit(solution)/shard_map/across_4/pallas_call | solution.py:419
  317.9 24.8 %across_7.1 = (f32[128,1152]{1,0:T(8,128)}, bf16[512,1152]{1,0:T(8,128)(2,1)}) custom-call(bf16[512,1152]{1,0:T(8,128)(2,1)} %convolution_convert_fusion.11.refs_0_, f32[128,1152]{1,0:T(8,128)} %get-tuple-element.105.refs_1_, f32[1,1152]{1,0:T(1,128)} %get-tuple-element.291.refs_2_, f32[1,1152]{1,0:T(1,128)} %get-tuple-element.290.refs_3_.refs_2_), custom_call_target="tpu_custom_call" | custom-call | tf_op jit(solution)/shard_map/across_7/pallas_call | solution.py:419
  348.1 39.2 %all-gather.30.cloned.1.call-done = bf16[1152,1152]{1,0:T(8,128)(2,1)} async-done(((bf16[144,1152]{1,0:T(8,128)(2,1)}), bf16[1152,1152]{1,0:T(8,128)(2,1)}) %all-gather.30.cloned.1.call-update) | async-done | bytes 2654224 | tf_op jit(solution)/shard_map/all_gather | solution.py:507
  392.9 15.2 %across_8.1 = (f32[128,1152]{1,0:T(8,128)}, f32[128,1152]{1,0:T(8,128)}, bf16[128,1152]{1,0:T(8,128)(2,1)}) custom-call(bf16[512,1152]{1,0:T(8,128)(2,1)} %convolution_convert_fusion.10.refs_0_, f32[128,1152]{1,0:T(8,128)} %get-tuple-element.107.refs_1_, f32[1,1152]{1,0:T(1,128)} %get-tuple-element.288.refs_2_, f32[1,1152]{1,0:T(1,128)} %get-tuple-element.295.refs_3_, ...), custom_call_target="tpu_custom_call" | custom-call | tf_op jit(solution)/shard_map/across_8/pallas_call | solution.py:419
  420.5 12.4 across_9.1
  442.5 25.2 %across_10.1 = (f32[128,1152]{1,0:T(8,128)}, f32[8,1152]{1,0:T(8,128)}, f32[8,1152]{1,0:T(8,128)}, bf16[512,1152]{1,0:T(8,128)(2,1)}) custom-call(bf16[512,1152]{1,0:T(8,128)(2,1)} %convolution_convert_fusion.9.refs_0_, f32[128,1152]{1,0:T(8,128)} %get-tuple-element.107.refs_1_, f32[1,1152]{1,0:T(1,128)} %get-tuple-element.290.refs_3_.refs_2_, ...), custom_call_target="tpu_custom_call" | custom-call | tf_op jit(solution)/shard_map/across_10/pallas_call | solution.py:419
  480.8 23.7 %across_11.1 = (f32[128,1152]{1,0:T(8,128)}, f32[8,1152]{1,0:T(8,128)}, bf16[512,1152]{1,0:T(8,128)(2,1)}) custom-call(bf16[512,1152]{1,0:T(8,128)(2,1)} %convolution_convert_fusion.8.refs_0_, f32[128,1152]{1,0:T(8,128)} %get-tuple-element.112.refs_1_, f32[128,1152]{1,0:T(8,128)} %get-tuple-element.113.refs_2_, f32[1,1152]{1,0:T(1,128)} %get-tuple-element.292.refs_2_.refs_3_), custom_call_target="tpu_custom_call" | custom-call | tf_op jit(solution)/shard_map/across_11/pallas_call | solution.py:419
  531.7 23.4 %across_12.1 = (f32[128,1152]{1,0:T(8,128)}, f32[8,1152]{1,0:T(8,128)}, bf16[512,1152]{1,0:T(8,128)(2,1)}) custom-call(bf16[512,1152]{1,0:T(8,128)(2,1)} %convolution_convert_fusion.7.refs_0_, f32[128,1152]{1,0:T(8,128)} %get-tuple-element.115.refs_1_, f32[128,1152]{1,0:T(8,128)} %get-tuple-element.116.refs_2_, f32[1,1152]{1,0:T(1,128)} %get-tuple-element.292.refs_2_.refs_3_), custom_call_target="tpu_custom_call" | custom-call | tf_op jit(solution)/shard_map/across_12/pallas_call | solution.py:419
  627.5 15.6 %across_13.1 = bf16[256,1152]{1,0:T(8,128)(2,1)} custom-call(bf16[256,1152]{1,0:T(8,128)(2,1)} %bitcast.375), custom_call_target="tpu_custom_call" | custom-call | tf_op jit(solution)/shard_map/across_13/pallas_call | solution.py:419
  665.1 60.1 %reduce-scatter.21.cloned.1.call-done = bf16[144,1152]{1,0:T(8,128)(2,1)} async-done(((bf16[1152,1152]{1,0:T(8,128)(2,1)}), bf16[144,1152]{1,0:T(8,128)(2,1)}) %reduce-scatter.21.cloned.1.call-update) | async-done | bytes 331792 | tf_op jit(solution)/shard_map/reduce_scatter | solution.py:702
  734.2 66.0 %reduce-scatter.23.cloned.1.call-done = bf16[144,1152]{1,0:T(8,128)(2,1)} async-done(((bf16[1152,1152]{1,0:T(8,128)(2,1)}), bf16[144,1152]{1,0:T(8,128)(2,1)}) %reduce-scatter.23.cloned.1.call-update) | async-done | bytes 331792 | tf_op jit(solution)/shard_map/reduce_scatter | solution.py:702
  809.6 15.7 %across_14.1 = (bf16[128,1152]{1,0:T(8,128)(2,1)}, f32[8,1152]{1,0:T(8,128)}, f32[8,1152]{1,0:T(8,128)}) custom-call(bf16[512,1152]{1,0:T(8,128)(2,1)} %convolution_convert_fusion.6.refs_0_, f32[128,1152]{1,0:T(8,128)} %constant_dynamic-slice_fusion.5.refs_1_, f32[1,1152]{1,0:T(1,128)} %get-tuple-element.287.refs_2_, f32[128,1152]{1,0:T(8,128)} %get-tuple-element.118.refs_3_), custom_call_target="tpu_custom_call" | custom-call | tf_op jit(solution)/shard_map/across_14/pallas_call | solution.py:419
  829.2 45.2 %reduce-scatter.15.cloned.1.call-done = bf16[144,1152]{1,0:T(8,128)(2,1)} async-done(((bf16[1152,1152]{1,0:T(8,128)(2,1)}), bf16[144,1152]{1,0:T(8,128)(2,1)}) %reduce-scatter.15.cloned.1.call-update) | async-done | bytes 331792 | tf_op jit(solution)/shard_map/reduce_scatter | solution.py:702
  890.9 19.6 %exchange_dp_16.1 = (bf16[8,16,1152]{2,1,0:T(8,128)(2,1)}, bf16[8,12,1152]{2,1,0:T(8,128)(2,1)}) custom-call(bf16[16,1152]{1,0:T(8,128)(2,1)} %reduce_sum.520.refs_0_, bf16[12,1152]{1,0:T(8,128)(2,1)} %reduce_sum.521.refs_1_), custom_call_target="tpu_custom_call" | custom-call | tf_op jit(solution)/shard_map/exchange_dp_16/pallas_call | solution.py:252
  915.4 19.5 %exchange_dp_17.1 = bf16[8,16,144]{2,1,0:T(8,128)(2,1)} custom-call(bf16[16,144]{1,0:T(8,128)(2,1)} %fusion.140.refs_0_), custom_call_target="tpu_custom_call" | custom-call | tf_op jit(solution)/shard_map/exchange_dp_17/pallas_call | solution.py:252
  967.3 81.7 %reduce-scatter.25.cloned.1.call-done = bf16[656,288]{1,0:T(8,128)(2,1)} async-done(((bf16[5248,288]{1,0:T(8,128)(2,1)}), bf16[656,288]{1,0:T(8,128)(2,1)}) %reduce-scatter.25.cloned.1.call-update) | async-done | bytes 377872
  1051.1 17.4 %all-gather.32.cloned.1.call-done = bf16[576,1152]{1,0:T(8,128)(2,1)} async-done(((bf16[144,1152]{1,0:T(8,128)(2,1)}), bf16[576,1152]{1,0:T(8,128)(2,1)}) %all-gather.32.cloned.1.call-update) | async-done | bytes 1327120 | tf_op jit(solution)/shard_map/all_gather | solution.py:890
  1203.9 16.1 %exchange_dp_20.1 = bf16[8,29,1152]{2,1,0:T(8,128)(2,1)} custom-call(bf16[29,1152]{1,0:T(8,128)(2,1)} %pad_maximum_fusion.12.refs_0_), custom_call_target="tpu_custom_call" | custom-call | tf_op jit(solution)/shard_map/exchange_dp_20/pallas_call | solution.py:252
  1273.9 20.9 %fusion.187 = (bf16[20,144,1152]{2,1,0:T(8,128)(2,1)}, f32[20,144,1152]{2,1,0:T(8,128)}, f32[20,144,1152]{2,1,0:T(8,128)}) fusion(f32[20,144,1152]{2,1,0:T(8,128)} %param.31, f32[20]{0:T(128)S(1)} %multiply_bitcast_fusion.1, f32[20]{0:T(128)S(1)} %maximum_bitcast_fusion.6, f32[20]{0:T(128)S(1)} %slice_bitcast_fusion.6, f32[20,1152]{1,0:T(8,128)S(1)} %fusion.128, ...), kind=kLoop, calls=%fused_computation.422 | loop fusion | flops 26542080 | bytes 59823604 | tf_op jit(solution)/shard_map/convert_element_type | solution.py:193
  (681 shorter events, 604.4 us)
Async XLA Ops:
  7.2 275.6 %copy-start = (bf16[2,120,4096]{2,1,0:T(8,128)(2,1)S(1)}, bf16[2,120,4096]{2,1,0:T(8,128)(2,1)}, u32[]{:S(2)}) copy-start(bf16[2,120,4096]{2,1,0:T(8,128)(2,1)} %param.30) | copy-start | bytes 5898244
  7.2 127.0 %all-gather.22.cloned.1.call-start = ((), (), s32[]{:S(2)}) async-start(), calls=%async_computation.6 | async-start | bytes 2985984 | tf_op jit(solution)/shard_map/all_gather | solution.py:502
  27.1 145.8 %all-gather.24.cloned.1.call-start = ((), (), s32[]{:S(2)}) async-start(), calls=%async_computation.7 | async-start | bytes 2985984 | tf_op jit(solution)/shard_map/all_gather | solution.py:503
  31.2 191.9 %all-gather.26.cloned.1.call-start = ((), (), s32[]{:S(2)}) async-start(), calls=%async_computation.8 | async-start | bytes 2985984 | tf_op jit(solution)/shard_map/all_gather | solution.py:505
  37.1 238.8 %all-gather.42.cloned.1.call-start = ((), (), s32[]{:S(2)}) async-start(), calls=%async_computation.18 | async-start | bytes 3981312 | tf_op jit(solution)/shard_map/all_gather | solution.py:504
  42.2 300.5 %all-gather.28.cloned.1.call-start = ((), (), s32[]{:S(2)}) async-start(), calls=%async_computation.9 | async-start | bytes 2985984 | tf_op jit(solution)/shard_map/all_gather | solution.py:506
  45.5 341.8 %all-gather.30.cloned.1.call-start = ((), (), s32[]{:S(2)}) async-start(), calls=%async_computation.10 | async-start | bytes 2985984 | tf_op jit(solution)/shard_map/all_gather | solution.py:507
  49.5 614.9 %reduce-scatter.19.cloned.1.call-start = ((), (), s32[]{:S(2)}) async-start(), calls=%async_computation.20 | async-start | bytes 2985984 | tf_op jit(solution)/shard_map/reduce_scatter | solution.py:702
  88.6 823.3 %copy-start.75 = (f32[16,144]{1,0:T(8,128)}, f32[16,144]{1,0:T(8,128)S(1)}, u32[]{:S(2)}) copy-start(f32[16,144]{1,0:T(8,128)S(1)} %reduce_sum.496) | copy-start | bytes 27652
  580.1 145.1 %reduce-scatter.21.cloned.1.call-start = ((), (), s32[]{:S(2)}) async-start(), calls=%async_computation.21 | async-start | bytes 2985984 | tf_op jit(solution)/shard_map/reduce_scatter | solution.py:702
  592.1 208.2 %reduce-scatter.23.cloned.1.call-start = ((), (), s32[]{:S(2)}) async-start(), calls=%async_computation.22 | async-start | bytes 2985984 | tf_op jit(solution)/shard_map/reduce_scatter | solution.py:702
  611.0 263.4 %reduce-scatter.15.cloned.1.call-start = ((), (), s32[]{:S(2)}) async-start(), calls=%async_computation.11 | async-start | bytes 2985984 | tf_op jit(solution)/shard_map/reduce_scatter | solution.py:702
  616.8 343.9 %reduce-scatter.17.cloned.1.call-start = ((), (), s32[]{:S(2)}) async-start(), calls=%async_computation.12 | async-start | bytes 2985984 | tf_op jit(solution)/shard_map/reduce_scatter | solution.py:702
  623.1 425.9 %reduce-scatter.25.cloned.1.call-start = ((), (), s32[]{:S(2)}) async-start(), calls=%async_computation.23 | async-start | bytes 4534272
  664.3 404.2 %all-gather.32.cloned.1.call-start = ((), (), s32[]{:S(2)}) async-start(), calls=%async_computation.13 | async-start | bytes 1658880 | tf_op jit(solution)/shard_map/all_gather | solution.py:890
  665.0 423.2 %all-gather.34.cloned.1.call-start = ((), (), s32[]{:S(2)}) async-start(), calls=%async_computation.14 | async-start | bytes 1658880 | tf_op jit(solution)/shard_map/all_gather | solution.py:890
  725.2 382.8 %all-gather.36.cloned.1.call-start = ((), (), s32[]{:S(2)}) async-start(), calls=%async_computation.15 | async-start | bytes 1658880 | tf_op jit(solution)/shard_map/all_gather | solution.py:890
  800.3 327.3 %all-gather.38.cloned.1.call-start = ((), (), s32[]{:S(2)}) async-start(), calls=%async_computation.16 | async-start | bytes 1658880 | tf_op jit(solution)/shard_map/all_gather | solution.py:890
  874.5 291.3 %all-gather.40.cloned.1.call-start = ((), (), s32[]{:S(2)}) async-start(), calls=%async_computation.17 | async-start | bytes 1658880 | tf_op jit(solution)/shard_map/all_gather | solution.py:890
  955.9 95.1 %copy-start.9 = (f32[256,1152]{1,0:T(8,128)}, f32[256,1152]{1,0:T(8,128)S(1)}, u32[]{:S(2)}) copy-start(f32[256,1152]{1,0:T(8,128)S(1)} %fusion.153) | copy-start | bytes 3538948
  960.8 234.3 %all-gather.44.cloned.1.call-start = ((), (), s32[]{:S(2)}) async-start(), calls=%async_computation.19 | async-start | bytes 2211840 | tf_op jit(solution)/shard_map/all_gather | solution.py:890
  961.1 112.4 %copy-start.41 = (f32[32,1152]{1,0:T(8,128)}, f32[32,1152]{1,0:T(8,128)S(1)}, u32[]{:S(2)}) copy-start(f32[32,1152]{1,0:T(8,128)S(1)} %get-tuple-element.285) | copy-start | bytes 442372
  962.0 340.5 %copy-start.112 = (f32[312]{0:T(512)}, f32[312]{0:T(512)S(1)}, u32[]{:S(2)}) copy-start(f32[312]{0:T(512)S(1)} %get-tuple-element.245) | copy-start | bytes 3748
  962.0 111.6 %copy-start.85 = (f32[1152]{0:T(1024)}, f32[1152]{0:T(1024)S(1)}, u32[]{:S(2)}) copy-start(f32[1152]{0:T(1024)S(1)} %multiply_add_fusion.5) | copy-start | bytes 13828
  (129 other events, 1609.8 us)
Sparse Core Ops, SparseCore 0:
  27.2 62.8 all-gather.21
  92.8 60.8 all-gather.23
  156.4 53.5 all-gather.25
  212.7 63.1 all-gather.41
  277.9 53.6 all-gather.27
  333.6 53.5 all-gather.29
  580.2 70.0 reduce-scatter.18
  654.5 70.6 reduce-scatter.20
  729.4 70.7 reduce-scatter.22
  803.7 70.6 reduce-scatter.14
  878.7 81.9 reduce-scatter.16
  964.8 84.1 reduce-scatter.24
  1050.6 17.8 all-gather.31
  1069.9 18.2 all-gather.33
  1089.6 18.2 all-gather.35
  1109.4 18.2 all-gather.37
  1129.0 18.2 all-gather.39
  1149.3 20.7 all-gather.43

commit v3 on v2

--- a/solution.py
+++ b/solution.py
@@ -886,15 +886,15 @@
     small_part = exchange("mp", [small_own], [True], 19)[0].reshape(mp_size * small_count, D)
     sum_small = jnp.concatenate([small_part[0:16], grad_freq, grad_tables, small_part[16:]], axis=0)
 
-    def all_columns(rows):
-        blocks = lax.all_gather(rows, "mp", axis=0, tiled=False)
+    def all_columns(rows, number):
+        blocks = exchange("mp", [rows], [True], number)[0]
         kinds = rows.shape[1] // lw
         stacked = blocks.reshape(mp_size, rows.shape[0], kinds, lw)
         return stacked.transpose(2, 1, 0, 3).reshape(kinds, rows.shape[0], mp_size * lw)
 
     whole_s, whole_t, whole_c, whole_i, whole_o, whole_x = [
-        all_columns(rows).astype(jnp.float32)
-        for rows in (sum_s, sum_t, sum_c, sum_i, sum_o, sum_x)
+        all_columns(rows, 22 + at).astype(jnp.float32)
+        for at, rows in enumerate((sum_s, sum_t, sum_c, sum_i, sum_o, sum_x))
     ]
     sum_in = jnp.concatenate(
         [whole_s[0:3], whole_t[0:3], whole_c[0:3], whole_i, grad_time, grad_temb_part[None]], axis=0

time: 1330 us -> 1220 us (0.917)
  waiting for transfers between devices: 374 us -> 141 us
  Pallas kernels: 356 us -> 466 us
    reduce_scatter x5 -> x6, waiting for transfers between devices: 176 us -> 56.8 us  [row_sum(): lax.psum_scatter(pieces.astype(bfloat), 'dp', scatter_dimension=0, tiled=...]
    pallas_call x10 -> x16, Pallas kernels: 137 us -> 247 us  [exchange(): pl.pallas_call(kernel, out_shape=shapes, in_specs=[vmem] * count, out_spe...]
    unnamed x19 -> x12, waiting for transfers between devices: 82.7 us -> 0.2 us
    all_gather x6 -> x0, waiting for transfers between devices: 31 us -> none  [all_columns(): blocks = lax.all_gather(rows, 'mp', axis=0, tiled=False)]
    unnamed x295 -> x283, local copies, waits for them, and re-layouts: 74.3 us -> 44.8 us
    convert_element_type x9 -> x10, local copies, waits for them, and re-layouts: 47.7 us -> 53.4 us  [shards(): all_columns(rows, 22 + at).astype(jnp.float32)]
  transfers between devices with their start and end apart: 18 -> 12, of which waited for: 11 -> 5; matrix products, arithmetic and copies ran while one was open for 27% -> 29% of each run, Pallas kernels for 17% -> 26%
where the time goes in v3:
time: 1220 us; the launch traced here: 1210 us
  Pallas kernels  466 us (38%)
  local copies, waits for them, and re-layouts  290 us (24%)
  other arithmetic  150 us (12%)
  waiting for transfers between devices  141 us (12%)
  matrix products  138 us (11%)
  between operations  24.2 us (2%)
    pallas_call x16, Pallas kernels, exchange(): pl.pallas_call(kernel, out_shape=shapes, in_specs=[vmem] * count, out_spe...  247 us
    pallas_call x11, Pallas kernels, across(): pl.pallas_call(kernel, out_shape=shapes, in_specs=[vmem] * len(inputs), o...  219 us
    dot_general x49, matrix products, contract(): return jnp.einsum(form, left, right, preferred_element_type=jnp.float32)  99.5 us
    reduce_scatter x6, waiting for transfers between devices, row_sum(): lax.psum_scatter(pieces.astype(bfloat), 'dp', scatter_dimension=0, tiled=...  56.8 us
    convert_element_type x10, local copies, waits for them, and re-layouts, shards(): all_columns(rows, 22 + at).astype(jnp.float32)  53.4 us
    all_gather x1, waiting for transfers between devices, shards(): full_x = lax.all_gather(pack_x, 'dp', axis=0, tiled=False)  45.4 us
    unnamed x283, local copies, waits for them, and re-layouts  44.8 us
    all_gather x1, waiting for transfers between devices, shards(): full_o = lax.all_gather(pack_o, 'dp', axis=0, tiled=True)  39.1 us
  transfers between devices with their start and end apart: 12, of which 5 were waited for; matrix products, arithmetic and copies ran while one was open for 29% of the time, Pallas kernels for 26%

profile of v3, /device:TPU:0, one launch (start us, length us, event | category | flops | bytes accessed | tf_op | source)
XLA Modules:
  0.0 1211.3 jit_solution(13400092482561433379)
XLA Ops:
  92.1 23.4 %exchange_dp_3.1 = f32[8,12,1152]{2,1,0:T(8,128)} custom-call(f32[8,12,1152]{2,1,0:T(8,128)} %reshape.883.refs_0_), custom_call_target="tpu_custom_call" | custom-call | tf_op jit(solution)/shard_map/exchange_dp_3/pallas_call | solution.py:252
  149.4 23.4 %across_5.1 = (f32[128,1152]{1,0:T(8,128)}, f32[128,1152]{1,0:T(8,128)}, bf16[512,1152]{1,0:T(8,128)(2,1)}) custom-call(bf16[512,1152]{1,0:T(8,128)(2,1)} %convolution_convert_fusion.13.refs_0_, f32[128,1152]{1,0:T(8,128)} %constant_dynamic-slice_fusion.5.refs_1_, f32[1,1152]{1,0:T(1,128)} %get-tuple-element.314.refs_2_.refs_3_, f32[128,1152]{1,0:T(8,128)} %bitcast.369), custom_call_target="tpu_custom_call" | custom-call | tf_op jit(solution)/shard_map/across_5/pallas_call | solution.py:419
  199.3 23.6 %across_6.1 = (f32[128,1152]{1,0:T(8,128)}, f32[128,1152]{1,0:T(8,128)}, bf16[512,1152]{1,0:T(8,128)(2,1)}) custom-call(bf16[512,1152]{1,0:T(8,128)(2,1)} %convolution_convert_fusion.12.refs_0_, f32[128,1152]{1,0:T(8,128)} %get-tuple-element.103.refs_1_, f32[1,1152]{1,0:T(1,128)} %get-tuple-element.314.refs_2_.refs_3_), custom_call_target="tpu_custom_call" | custom-call | tf_op jit(solution)/shard_map/across_6/pallas_call | solution.py:419
  230.5 45.4 %all-gather.19.cloned.1.call-done = bf16[8,656,288]{1,2,0:T(8,128)(2,1)} async-done(((bf16[1,656,288]{1,2,0:T(8,128)(2,1)}), bf16[8,656,288]{1,2,0:T(8,128)(2,1)}) %all-gather.19.cloned.1.call-update) | async-done | bytes 3022864 | tf_op jit(solution)/shard_map/all_gather | solution.py:504
  285.4 15.9 %across_4.1 = bf16[256,1152]{1,0:T(8,128)(2,1)} custom-call(bf16[256,1152]{1,0:T(8,128)(2,1)} %bitcast.368), custom_call_target="tpu_custom_call" | custom-call | tf_op jit(solution)/shard_map/across_4/pallas_call | solution.py:419
  318.0 24.8 %across_7.1 = (f32[128,1152]{1,0:T(8,128)}, bf16[512,1152]{1,0:T(8,128)(2,1)}) custom-call(bf16[512,1152]{1,0:T(8,128)(2,1)} %convolution_convert_fusion.11.refs_0_, f32[128,1152]{1,0:T(8,128)} %get-tuple-element.105.refs_1_, f32[1,1152]{1,0:T(1,128)} %get-tuple-element.313.refs_2_, f32[1,1152]{1,0:T(1,128)} %get-tuple-element.312.refs_3_.refs_2_), custom_call_target="tpu_custom_call" | custom-call | tf_op jit(solution)/shard_map/across_7/pallas_call | solution.py:419
  348.2 39.1 %all-gather.17.cloned.1.call-done = bf16[1152,1152]{1,0:T(8,128)(2,1)} async-done(((bf16[144,1152]{1,0:T(8,128)(2,1)}), bf16[1152,1152]{1,0:T(8,128)(2,1)}) %all-gather.17.cloned.1.call-update) | async-done | bytes 2654224 | tf_op jit(solution)/shard_map/all_gather | solution.py:507
  393.0 15.3 %across_8.1 = (f32[128,1152]{1,0:T(8,128)}, f32[128,1152]{1,0:T(8,128)}, bf16[128,1152]{1,0:T(8,128)(2,1)}) custom-call(bf16[512,1152]{1,0:T(8,128)(2,1)} %convolution_convert_fusion.10.refs_0_, f32[128,1152]{1,0:T(8,128)} %get-tuple-element.107.refs_1_, f32[1,1152]{1,0:T(1,128)} %get-tuple-element.310.refs_2_, f32[1,1152]{1,0:T(1,128)} %get-tuple-element.317.refs_3_, ...), custom_call_target="tpu_custom_call" | custom-call | tf_op jit(solution)/shard_map/across_8/pallas_call | solution.py:419
  442.7 25.1 %across_10.1 = (f32[128,1152]{1,0:T(8,128)}, f32[8,1152]{1,0:T(8,128)}, f32[8,1152]{1,0:T(8,128)}, bf16[512,1152]{1,0:T(8,128)(2,1)}) custom-call(bf16[512,1152]{1,0:T(8,128)(2,1)} %convolution_convert_fusion.9.refs_0_, f32[128,1152]{1,0:T(8,128)} %get-tuple-element.107.refs_1_, f32[1,1152]{1,0:T(1,128)} %get-tuple-element.312.refs_3_.refs_2_, ...), custom_call_target="tpu_custom_call" | custom-call | tf_op jit(solution)/shard_map/across_10/pallas_call | solution.py:419
  480.9 23.7 %across_11.1 = (f32[128,1152]{1,0:T(8,128)}, f32[8,1152]{1,0:T(8,128)}, bf16[512,1152]{1,0:T(8,128)(2,1)}) custom-call(bf16[512,1152]{1,0:T(8,128)(2,1)} %convolution_convert_fusion.8.refs_0_, f32[128,1152]{1,0:T(8,128)} %get-tuple-element.112.refs_1_, f32[128,1152]{1,0:T(8,128)} %get-tuple-element.113.refs_2_, f32[1,1152]{1,0:T(1,128)} %get-tuple-element.314.refs_2_.refs_3_), custom_call_target="tpu_custom_call" | custom-call | tf_op jit(solution)/shard_map/across_11/pallas_call | solution.py:419
  531.7 23.5 %across_12.1 = (f32[128,1152]{1,0:T(8,128)}, f32[8,1152]{1,0:T(8,128)}, bf16[512,1152]{1,0:T(8,128)(2,1)}) custom-call(bf16[512,1152]{1,0:T(8,128)(2,1)} %convolution_convert_fusion.7.refs_0_, f32[128,1152]{1,0:T(8,128)} %get-tuple-element.115.refs_1_, f32[128,1152]{1,0:T(8,128)} %get-tuple-element.116.refs_2_, f32[1,1152]{1,0:T(1,128)} %get-tuple-element.314.refs_2_.refs_3_), custom_call_target="tpu_custom_call" | custom-call | tf_op jit(solution)/shard_map/across_12/pallas_call | solution.py:419
  661.1 15.8 %across_13.1 = bf16[256,1152]{1,0:T(8,128)(2,1)} custom-call(bf16[256,1152]{1,0:T(8,128)(2,1)} %bitcast.367), custom_call_target="tpu_custom_call" | custom-call | tf_op jit(solution)/shard_map/across_13/pallas_call | solution.py:419
  692.0 15.7 %across_14.1 = (bf16[128,1152]{1,0:T(8,128)(2,1)}, f32[8,1152]{1,0:T(8,128)}, f32[8,1152]{1,0:T(8,128)}) custom-call(bf16[512,1152]{1,0:T(8,128)(2,1)} %convolution_convert_fusion.6.refs_0_, f32[128,1152]{1,0:T(8,128)} %constant_dynamic-slice_fusion.5.refs_1_, f32[1,1152]{1,0:T(1,128)} %get-tuple-element.309.refs_2_, f32[128,1152]{1,0:T(8,128)} %get-tuple-element.118.refs_3_), custom_call_target="tpu_custom_call" | custom-call | tf_op jit(solution)/shard_map/across_14/pallas_call | solution.py:419
  727.3 17.9 %exchange_dp_16.1 = (bf16[8,16,1152]{2,1,0:T(8,128)(2,1)}, bf16[8,12,1152]{2,1,0:T(8,128)(2,1)}) custom-call(bf16[16,1152]{1,0:T(8,128)(2,1)} %reduce_sum.520.refs_0_, bf16[12,1152]{1,0:T(8,128)(2,1)} %reduce_sum.521.refs_1_), custom_call_target="tpu_custom_call" | custom-call | tf_op jit(solution)/shard_map/exchange_dp_16/pallas_call | solution.py:252
  795.1 19.1 %exchange_mp_22.1 = bf16[4,144,1152]{2,1,0:T(8,128)(2,1)} custom-call(bf16[144,1152]{1,0:T(8,128)(2,1)} %reduce-scatter.7.cloned.1.call-done.refs_0_), custom_call_target="tpu_custom_call" | custom-call | tf_op jit(solution)/shard_map/exchange_mp_22/pallas_call | solution.py:252
  823.4 19.1 %exchange_mp_23.1 = bf16[4,144,1152]{2,1,0:T(8,128)(2,1)} custom-call(bf16[144,1152]{1,0:T(8,128)(2,1)} %reduce-scatter.9.cloned.1.call-done.refs_0_), custom_call_target="tpu_custom_call" | custom-call | tf_op jit(solution)/shard_map/exchange_mp_23/pallas_call | solution.py:252
  851.3 19.1 %exchange_mp_24.1 = bf16[4,144,1152]{2,1,0:T(8,128)(2,1)} custom-call(bf16[144,1152]{1,0:T(8,128)(2,1)} %reduce-scatter.11.cloned.1.call-done.refs_0_), custom_call_target="tpu_custom_call" | custom-call | tf_op jit(solution)/shard_map/exchange_mp_24/pallas_call | solution.py:252
  879.1 16.6 %reduce-scatter.15.cloned.1.call-done.refs_0_ = bf16[144,1152]{1,0:T(8,128)(2,1)} async-done(((bf16[1152,1152]{1,0:T(8,128)(2,1)}), bf16[144,1152]{1,0:T(8,128)(2,1)}) %reduce-scatter.15.cloned.1.call-update) | async-done | bytes 331792 | tf_op jit(solution)/shard_map/reduce_scatter | solution.py:702
  895.7 18.3 %exchange_mp_26.1 = bf16[4,144,1152]{2,1,0:T(8,128)(2,1)} custom-call(bf16[144,1152]{1,0:T(8,128)(2,1)} %reduce-scatter.15.cloned.1.call-done.refs_0_), custom_call_target="tpu_custom_call" | custom-call | tf_op jit(solution)/shard_map/exchange_mp_26/pallas_call | solution.py:252
  969.5 18.3 %exchange_mp_25.1 = bf16[4,144,1152]{2,1,0:T(8,128)(2,1)} custom-call(bf16[144,1152]{1,0:T(8,128)(2,1)} %reduce-scatter.13.cloned.1.call-done.refs_0_), custom_call_target="tpu_custom_call" | custom-call | tf_op jit(solution)/shard_map/exchange_mp_25/pallas_call | solution.py:252
  1030.0 28.1 %reduce-scatter.17.cloned.1.call-done.refs_0_ = bf16[656,288]{1,0:T(8,128)(2,1)} async-done(((bf16[5248,288]{1,0:T(8,128)(2,1)}), bf16[656,288]{1,0:T(8,128)(2,1)}) %reduce-scatter.17.cloned.1.call-update) | async-done | bytes 377872 | tf_op jit(solution)/shard_map/reduce_scatter | solution.py:702
  1058.2 25.9 %exchange_mp_27.1 = bf16[4,656,288]{2,1,0:T(8,128)(2,1)} custom-call(bf16[656,288]{1,0:T(8,128)(2,1)} %reduce-scatter.17.cloned.1.call-done.refs_0_), custom_call_target="tpu_custom_call" | custom-call | tf_op jit(solution)/shard_map/exchange_mp_27/pallas_call | solution.py:252
  1101.9 15.3 %exchange_dp_20.1 = bf16[8,29,1152]{2,1,0:T(8,128)(2,1)} custom-call(bf16[29,1152]{1,0:T(8,128)(2,1)} %pad_maximum_fusion.11.refs_0_), custom_call_target="tpu_custom_call" | custom-call | tf_op jit(solution)/shard_map/exchange_dp_20/pallas_call | solution.py:252
  1171.1 20.9 %fusion.188 = (bf16[20,144,1152]{2,1,0:T(8,128)(2,1)}, f32[20,144,1152]{2,1,0:T(8,128)}, f32[20,144,1152]{2,1,0:T(8,128)}) fusion(f32[20,144,1152]{2,1,0:T(8,128)} %param.31, f32[20]{0:T(128)S(1)} %multiply_bitcast_fusion.1, f32[20]{0:T(128)S(1)} %maximum_bitcast_fusion.6, f32[20]{0:T(128)S(1)} %slice_bitcast_fusion.6, f32[20,1152]{1,0:T(8,128)S(1)} %fusion.129, ...), kind=kLoop, calls=%fused_computation.422 | loop fusion | flops 26542080 | bytes 59823604 | tf_op jit(solution)/shard_map/convert_element_type | solution.py:193
  (665 shorter events, 653.5 us)
Async XLA Ops:
  7.2 275.6 %copy-start = (bf16[2,120,4096]{2,1,0:T(8,128)(2,1)S(1)}, bf16[2,120,4096]{2,1,0:T(8,128)(2,1)}, u32[]{:S(2)}) copy-start(bf16[2,120,4096]{2,1,0:T(8,128)(2,1)} %param.30) | copy-start | bytes 5898244
  7.2 126.8 %all-gather.9.cloned.1.call-start = ((), (), s32[]{:S(2)}) async-start(), calls=%async_computation.6 | async-start | bytes 2985984 | tf_op jit(solution)/shard_map/all_gather | solution.py:502
  27.1 145.8 %all-gather.11.cloned.1.call-start = ((), (), s32[]{:S(2)}) async-start(), calls=%async_computation.7 | async-start | bytes 2985984 | tf_op jit(solution)/shard_map/all_gather | solution.py:503
  31.2 191.7 %all-gather.13.cloned.1.call-start = ((), (), s32[]{:S(2)}) async-start(), calls=%async_computation.8 | async-start | bytes 2985984 | tf_op jit(solution)/shard_map/all_gather | solution.py:505
  37.1 238.8 %all-gather.19.cloned.1.call-start = ((), (), s32[]{:S(2)}) async-start(), calls=%async_computation.17 | async-start | bytes 3981312 | tf_op jit(solution)/shard_map/all_gather | solution.py:504
  42.2 300.6 %all-gather.15.cloned.1.call-start = ((), (), s32[]{:S(2)}) async-start(), calls=%async_computation.9 | async-start | bytes 2985984 | tf_op jit(solution)/shard_map/all_gather | solution.py:506
  45.5 341.8 %all-gather.17.cloned.1.call-start = ((), (), s32[]{:S(2)}) async-start(), calls=%async_computation.10 | async-start | bytes 2985984 | tf_op jit(solution)/shard_map/all_gather | solution.py:507
  49.5 745.6 %reduce-scatter.7.cloned.1.call-start = ((), (), s32[]{:S(2)}) async-start(), calls=%async_computation.11 | async-start | bytes 2985984 | tf_op jit(solution)/shard_map/reduce_scatter | solution.py:702
  88.6 658.1 %copy-start.70 = (f32[16,144]{1,0:T(8,128)}, f32[16,144]{1,0:T(8,128)S(1)}, u32[]{:S(2)}) copy-start(f32[16,144]{1,0:T(8,128)S(1)} %reduce_sum.496) | copy-start | bytes 27652
  592.3 231.0 %reduce-scatter.9.cloned.1.call-start = ((), (), s32[]{:S(2)}) async-start(), calls=%async_computation.12 | async-start | bytes 2985984 | tf_op jit(solution)/shard_map/reduce_scatter | solution.py:702
  607.7 243.6 %reduce-scatter.11.cloned.1.call-start = ((), (), s32[]{:S(2)}) async-start(), calls=%async_computation.13 | async-start | bytes 2985984 | tf_op jit(solution)/shard_map/reduce_scatter | solution.py:702
  633.1 262.6 %reduce-scatter.15.cloned.1.call-start = ((), (), s32[]{:S(2)}) async-start(), calls=%async_computation.15 | async-start | bytes 2985984 | tf_op jit(solution)/shard_map/reduce_scatter | solution.py:702
  639.4 330.2 %reduce-scatter.13.cloned.1.call-start = ((), (), s32[]{:S(2)}) async-start(), calls=%async_computation.14 | async-start | bytes 2985984 | tf_op jit(solution)/shard_map/reduce_scatter | solution.py:702
  648.9 409.3 %reduce-scatter.17.cloned.1.call-start = ((), (), s32[]{:S(2)}) async-start(), calls=%async_computation.16 | async-start | bytes 4534272 | tf_op jit(solution)/shard_map/reduce_scatter | solution.py:702
  746.7 28.1 %copy-start.34 = (bf16[240,1152]{0,1:T(8,128)(2,1)S(1)}, bf16[240,1152]{0,1:T(8,128)(2,1)}, u32[]{:S(2)}) copy-start(bf16[240,1152]{0,1:T(8,128)(2,1)} %copy.503) | copy-start | bytes 1658884
  746.7 28.1 %copy-start.52 = (f32[240,288]{0,1:T(8,128)S(1)}, f32[240,288]{0,1:T(8,128)}, u32[]{:S(2)}) copy-start(f32[240,288]{0,1:T(8,128)} %copy-done.51) | copy-start | bytes 829444
  790.3 409.4 %copy-start.107 = (f32[312]{0:T(512)}, f32[312]{0:T(512)S(1)}, u32[]{:S(2)}) copy-start(f32[312]{0:T(512)S(1)} %get-tuple-element.267) | copy-start | bytes 3748
  790.3 29.3 %copy-start.80 = (f32[1152]{0:T(1024)}, f32[1152]{0:T(1024)S(1)}, u32[]{:S(2)}) copy-start(f32[1152]{0:T(1024)S(1)} %multiply_add_fusion.5) | copy-start | bytes 13828
  1025.7 145.4 %copy-start.72 = (f32[20,144]{1,0:T(8,128)}, f32[20,144]{1,0:T(8,128)S(1)}, u32[]{:S(2)}) copy-start(f32[20,144]{1,0:T(8,128)S(1)} %get-tuple-element.269) | copy-start | bytes 34564
  1118.4 39.5 %copy-start.77 = (f32[1152]{0:T(1024)}, f32[1152]{0:T(1024)S(1)}, u32[]{:S(2)}) copy-start(f32[1152]{0:T(1024)S(1)} %multiply_add_fusion.6) | copy-start | bytes 13828
  1119.0 38.8 %copy-start.100 = (f32[512]{0:T(512)}, f32[512]{0:T(512)S(1)}, u32[]{:S(2)}) copy-start(f32[512]{0:T(512)S(1)} %get-tuple-element.273) | copy-start | bytes 6148
  1124.3 67.8 %copy-start.67 = (f32[8,1152]{1,0:T(8,128)}, f32[8,1152]{1,0:T(8,128)S(1)}, u32[]{:S(2)}) copy-start(f32[8,1152]{1,0:T(8,128)S(1)} %fusion.136) | copy-start | bytes 110596
  1124.3 46.8 %copy-start.53 = (f32[20,1152]{1,0:T(8,128)}, f32[20,1152]{1,0:T(8,128)S(1)}, u32[]{:S(2)}) copy-start(f32[20,1152]{1,0:T(8,128)S(1)} %fusion.129) | copy-start | bytes 276484
  1124.5 67.6 %copy-start.79 = (f32[8,144]{1,0:T(8,128)}, f32[8,144]{1,0:T(8,128)S(1)}, u32[]{:S(2)}) copy-start(f32[8,144]{1,0:T(8,128)S(1)} %get-tuple-element.271) | copy-start | bytes 13828
  (120 other events, 876.9 us)
Sparse Core Ops, SparseCore 0:
  27.2 62.7 all-gather.8
  92.7 60.8 all-gather.10
  156.4 53.6 all-gather.12
  212.7 63.1 all-gather.18
  277.9 53.6 all-gather.14
  333.6 53.6 all-gather.16
  592.4 70.0 reduce-scatter.6
  666.8 78.5 reduce-scatter.8
  749.7 71.1 reduce-scatter.10
  825.0 70.6 reduce-scatter.14
  899.3 70.1 reduce-scatter.12
  973.6 84.5 reduce-scatter.16
